TPU v7x, 256 devices: a whole 4x4x8 slice. The times are simulated.
256 devices in a mesh: cohort: 8 (over z_lo, core), gene: 32 (over x, y, z_hi).
Axes of the slice: x: 4, y: 4, z: 8 (z_hi: 2, z_lo: 4; z = z_hi * 4 + z_lo), core: 2. Of those that a mesh axis runs over, the one named last changes fastest.
Arguments:
- expression: bfloat16 [24000, 3200], P('gene'), as said below
- sample_index: int32 [8, 400], P('cohort'), may hold values from 0 to 3199, as said below
- gene_block: int32 [24000], P('gene'), may hold values from 0 to 127
Outputs:
- connectivity: float32 [4864, 128], P(('cohort', 'gene'))
Inputs may be any that keep to these rules, and one draw needn't show every extreme that they name: `sample_index`: the entries together are a permutation of the 3200 pooled samples, 400 in each cohort. Finite expression values; genes of a module co-vary with a strength that differs between cohorts.
All inputs are finite; a program needn't handle non-finite values.
Results may differ from a plain program's by a relative error of at most 0.00097.
Values may be sent and summed in bfloat16 or wider, within the bound.
No kernel may reach another device: no remote copies, remote signals or barrier semaphores. Data moves between devices by JAX's collectives and lax.ppermute only.
A program may use at most 64 MiB of HBM per device.

v0:
```python
import jax
import jax.numpy as jnp
from jax import lax
from jax.sharding import Mesh
from jax.sharding import PartitionSpec as P

MODULES = 128
ROW_DEV = 152
GENE = ("gene_0", "gene_1", "gene_2")
COHORT_GENE = ("cohort", "gene_0", "gene_1", "gene_2")


def laid_out(parts, dim):
    dims = list(parts.shape[1:])
    dims[dim] *= parts.shape[0]
    return jnp.moveaxis(parts, 0, dim).reshape(dims)


def stacked_from(array, axes, turns):
    parts = array
    for k in turns:
        parts = lax.all_gather(parts, axes[k])
    done = turns[::-1]
    back = [done.index(k) for k in range(len(axes))]
    parts = parts.transpose(*back, *range(len(axes), parts.ndim))
    return parts.reshape(-1, *array.shape)


def whole_of(array, axes, turns, dim):
    return laid_out(stacked_from(array, axes, turns), dim)


def sent_to_all(array, axis):
    peers = lax.axis_size(axis)
    return lax.all_to_all(
        jnp.broadcast_to(array[None], (peers, *array.shape)), axis, 0, 0, tiled=True
    )


def gathered_copies(array, axis, dim):
    return laid_out(sent_to_all(array, axis), dim)


def in_blocks(array, dim, peers):
    dims = array.shape
    parts = array.reshape(*dims[:dim], peers, dims[dim] // peers, *dims[dim + 1 :])
    return jnp.moveaxis(parts, dim, 0)


def summed_on_arrival(array, axis, dim):
    parts = in_blocks(array, dim, lax.axis_size(axis))
    arrived = lax.all_to_all(parts, axis, split_axis=0, concat_axis=0, tiled=True)
    return arrived.sum(axis=0)


def standardize(block):
    values = block.astype(jnp.float32)
    centred = values - jnp.mean(values, axis=1, keepdims=True)
    spread = jnp.sqrt(jnp.sum(centred * centred, axis=1, keepdims=True) + 0.01 * centred.shape[1])
    return (centred / spread).astype(jnp.bfloat16)


def power_twelve(corr):
    base = (1.0 + corr) * 0.5
    square = base * base
    fourth = square * square
    return (fourth * fourth * fourth).astype(jnp.bfloat16)


def on_device(expression, sample_index, gene_block):
    scores = standardize(jnp.take(expression, sample_index[0], axis=1))
    window_local = scores[:ROW_DEV]
    cohorts = lax.axis_size("cohort")
    width = ROW_DEV * lax.axis_size(GENE)
    share = width // cohorts
    window_all = whole_of(window_local, GENE, (2, 0, 1), 0)
    window_all = window_all.reshape(1, cohorts, share, window_all.shape[1])
    window_part = lax.all_to_all(window_all, "cohort", split_axis=1, concat_axis=0, tiled=True)
    window_part = window_part.reshape(cohorts, share, window_part.shape[3])
    all_lists = gathered_copies(sample_index, "cohort", 0)
    column_all = jnp.stack(
        [standardize(jnp.take(expression, all_lists[source], axis=1)) for source in range(cohorts)]
    )
    corr = jnp.einsum("cjs,cis->cji", column_all, window_part, preferred_element_type=jnp.float32)
    consensus = jnp.min(power_twelve(corr), axis=0)
    onehot = (gene_block[:, None] == jnp.arange(MODULES, dtype=jnp.int32)[None, :]).astype(
        jnp.bfloat16
    )
    partial_degree = lax.dot_general(
        consensus, onehot, (((0,), (0,)), ((), ())), preferred_element_type=jnp.float32
    )
    degree = summed_on_arrival(partial_degree, GENE, 0)
    return jnp.log1p(degree)


def solution(mesh):
    finer = Mesh(
        mesh.devices.reshape(mesh.shape["cohort"], 4, 4, 2),
        ("cohort", "gene_0", "gene_1", "gene_2"),
    )
    placed = (P(GENE, None), P("cohort", None), P(GENE))
    return jax.shard_map(
        on_device, mesh=finer, in_specs=placed, out_specs=P(COHORT_GENE, None), check_vma=False
    )
```

profile of v0, /device:TPU:1, one launch (start us, length us, event | category | flops | bytes accessed | tf_op | source)
XLA Modules:
  0.0 264.9 jit_solution(10731968006987624213)
XLA Ops:
  6.5 0.7 compare_select_fusion
  7.2 0.7 compare_and_fusion
  7.9 7.4 %copy.26 = bf16[750,3200]{0,1:T(8,128)(2,1)} copy(bf16[750,3200]{1,0:T(8,128)(2,1)} %param.5) | data formatting | bytes 9600000 | tf_op args[0]
  15.3 5.6 %gather_fusion.8 = bf16[400,750]{1,0:T(8,128)(2,1)S(1)} fusion(bf16[750,3200]{0,1:T(8,128)(2,1)} %copy.26, s32[1024]{0:T(1024)S(1)} %pad_clamp_fusion), kind=kCustom, calls=%fused_computation.8.clone | custom fusion | bytes 1201600 | tf_op jit(solution)/shard_map/jit(_take)/gather | solution.py:71
  21.6 11.7 %all-gather = bf16[304,400]{1,0:T(8,128)(2,1)S(1)} all-gather(bf16[152,400]{1,0:T(8,128)(2,1)S(1)} %copy.35), channel_id=2, replica_groups=mesh['cohort'=8,'gene_0'=4,'gene_1'=4,'gene_2'=2] {'gene_2'}, dimensions={0}, use_global_device_ids=true | all-gather | bytes 364800 | tf_op jit(solution)/shard_map/all_gather | solution.py:22
  33.3 15.3 %all-gather.1 = bf16[8,152,400]{2,1,0:T(8,128)(2,1)} all-gather(bf16[2,152,400]{2,1,0:T(8,128)(2,1)S(1)} %bitcast.98), channel_id=3, replica_groups=mesh['cohort'=8,'gene_0'=4,'gene_1'=4,'gene_2'=2] {'gene_0'}, dimensions={0}, use_global_device_ids=true | all-gather | bytes 1216000 | tf_op jit(solution)/shard_map/all_gather | solution.py:22
  48.7 14.6 %all_to_all.19 = s32[8,1,400]{2,1,0:T(1,128)S(1)} all-to-all(s32[8,1,400]{2,1,0:T(1,128)S(1)} %broadcast_in_dim.14), channel_id=1, replica_groups=mesh['cohort'=8,'gene_0'=4,'gene_1'=4,'gene_2'=2] {'cohort'}, dimensions={0} | all-to-all | bytes 25600 | tf_op jit(solution)/shard_map/all_to_all | solution.py:35
  63.3 5.6 %gather_fusion = bf16[400,750]{1,0:T(8,128)(2,1)S(1)} fusion(bf16[750,3200]{0,1:T(8,128)(2,1)} %copy.26, s32[1024]{0:T(1024)S(1)} %get-tuple-element.23), kind=kCustom, calls=%fused_computation.clone | custom fusion | bytes 1201600 | tf_op jit(solution)/shard_map/jit(_take)/gather | solution.py:82
  68.9 5.9 %gather_fusion.1 = bf16[400,750]{1,0:T(8,128)(2,1)S(1)} fusion(bf16[750,3200]{0,1:T(8,128)(2,1)} %copy.26, s32[1024]{0:T(1024)S(1)} %get-tuple-element.22), kind=kCustom, calls=%fused_computation.1.clone | custom fusion | bytes 1201600 | tf_op jit(solution)/shard_map/jit(_take)/gather | solution.py:82
  74.8 6.1 %gather_fusion.2 = bf16[400,750]{1,0:T(8,128)(2,1)} fusion(bf16[750,3200]{0,1:T(8,128)(2,1)} %copy.26, s32[1024]{0:T(1024)S(1)} %get-tuple-element.21), kind=kCustom, calls=%fused_computation.2.clone | custom fusion | bytes 1201600 | tf_op jit(solution)/shard_map/jit(_take)/gather | solution.py:82
  80.9 5.6 %gather_fusion.3 = bf16[400,750]{1,0:T(8,128)(2,1)S(1)} fusion(bf16[750,3200]{0,1:T(8,128)(2,1)} %copy.26, s32[1024]{0:T(1024)S(1)} %get-tuple-element.20), kind=kCustom, calls=%fused_computation.3.clone | custom fusion | bytes 1201600 | tf_op jit(solution)/shard_map/jit(_take)/gather | solution.py:82
  86.5 6.1 %gather_fusion.4 = bf16[400,750]{1,0:T(8,128)(2,1)} fusion(bf16[750,3200]{0,1:T(8,128)(2,1)} %copy.26, s32[1024]{0:T(1024)S(1)} %get-tuple-element.19), kind=kCustom, calls=%fused_computation.4.clone | custom fusion | bytes 1201600 | tf_op jit(solution)/shard_map/jit(_take)/gather | solution.py:82
  92.7 5.7 %gather_fusion.5 = bf16[400,750]{1,0:T(8,128)(2,1)S(1)} fusion(bf16[750,3200]{0,1:T(8,128)(2,1)} %copy.26, s32[1024]{0:T(1024)S(1)} %get-tuple-element.18), kind=kCustom, calls=%fused_computation.5.clone | custom fusion | bytes 1201600 | tf_op jit(solution)/shard_map/jit(_take)/gather | solution.py:82
  98.4 6.1 %gather_fusion.6 = bf16[400,750]{1,0:T(8,128)(2,1)} fusion(bf16[750,3200]{0,1:T(8,128)(2,1)} %copy.26, s32[1024]{0:T(1024)S(1)} %get-tuple-element.17), kind=kCustom, calls=%fused_computation.6.clone | custom fusion | bytes 1201600 | tf_op jit(solution)/shard_map/jit(_take)/gather | solution.py:82
  104.5 5.6 %gather_fusion.7 = bf16[400,750]{1,0:T(8,128)(2,1)S(1)} fusion(bf16[750,3200]{0,1:T(8,128)(2,1)} %copy.26, s32[1024]{0:T(1024)S(1)} %get-tuple-element.16), kind=kCustom, calls=%fused_computation.7.clone | custom fusion | bytes 1201600 | tf_op jit(solution)/shard_map/jit(_take)/gather | solution.py:82
  110.5 0.6 copy-done
  112.8 5.2 %copy.36 = bf16[4,4,2,152,400]{4,3,2,0,1:T(8,128)(2,1)} copy(bf16[4,4,2,152,400]{4,3,2,1,0:T(8,128)(2,1)} %bitcast.96) | data formatting | bytes 7782400 | tf_op jit(solution)/shard_map/all_gather | solution.py:22
  118.0 7.5 %copy.37 = bf16[1,8,608,400]{2,3,0,1:T(8,128)(2,1)} copy(bf16[1,8,608,400]{3,2,1,0:T(8,128)(2,1)} %bitcast.95) | data formatting | bytes 7782400 | tf_op jit(solution)/shard_map/reshape;reshape;reshape | solution.py:77
  125.5 5.3 %all-to-all-start.1 = ((bf16[1,8,608,400]{2,3,0,1:T(8,128)(2,1)}), bf16[1,8,608,400]{2,3,0,1:T(8,128)(2,1)}, u32[]{:S(2)}, u32[]{:S(2)}) async-start(bf16[1,8,608,400]{2,3,0,1:T(8,128)(2,1)} %copy.37), calls=%async_computation.1 | async-start | bytes 8192000 | tf_op jit(solution)/shard_map/all_to_all | solution.py:78
  133.8 1.1 fusion.38
  134.9 1.2 fusion.40
  136.1 1.1 fusion.42
  137.2 1.1 fusion.44
  138.3 1.1 fusion.46
  139.4 1.1 fusion.48
  140.4 1.1 fusion.50
  141.5 1.1 fusion.52
  142.6 79.2 %all-to-all-done.1 = bf16[1,8,608,400]{2,3,0,1:T(8,128)(2,1)} async-done(((bf16[1,8,608,400]{2,3,0,1:T(8,128)(2,1)}), bf16[1,8,608,400]{2,3,0,1:T(8,128)(2,1)}, u32[]{:S(2)}, u32[]{:S(2)}) %all-to-all-start.1) | async-done | bytes 3891232 | tf_op jit(solution)/shard_map/all_to_all | solution.py:78
  221.8 8.8 %fusion.2 = bf16[750,608]{0,1:T(8,128)(2,1)S(1)} fusion(bf16[8,750,400]{1,2,0:T(8,128)(2,1)} %fusion.52, bf16[1,8,608,400]{2,3,0,1:T(8,128)(2,1)} %all-to-all-done.1), kind=kOutput, calls=%fused_computation.12 | convolution fusion | flops 2947128064 | bytes 9603200 | tf_op jit(solution)/shard_map/cjs,cis->cji/dot_general | solution.py:84
  231.2 0.6 fusion.55
  231.8 25.6 %all_to_all.20 = f32[32,19,128]{2,1,0:T(8,128)S(1)} all-to-all(f32[32,19,128]{2,1,0:T(8,128)S(1)} %fusion.55), channel_id=1, replica_groups=mesh['cohort'=8,'gene_0'=4,'gene_1'=4,'gene_2'=2] {'gene_0','gene_1','ge..., dimensions={0} | all-to-all | bytes 622592 | tf_op jit(solution)/shard_map/all_to_all | solution.py:52
  257.4 0.6 log1p.3
  (82 shorter events, 6.4 us)
Async XLA Ops:
  6.5 106.2 %all-gather.5.cloned.1.call-start = ((), (), s32[]{:S(2)}) async-start(), calls=%async_computation.3 | async-start | bytes 6225920 | tf_op jit(solution)/shard_map/all_gather | solution.py:22
  33.3 15.4 %copy-start.6 = (s32[1,400]{1,0:T(1,128)S(1)}, s32[1,400]{1,0:T(1,128)}, u32[]{:S(2)}) copy-start(s32[1,400]{1,0:T(1,128)} %param.6) | copy-start | bytes 4804
  110.0 1.1 copy-start
  110.1 1.5 copy-start.2
  111.1 1.1 copy-start.4
  125.5 96.3 %all-to-all-start.1 = ((bf16[1,8,608,400]{2,3,0,1:T(8,128)(2,1)}), bf16[1,8,608,400]{2,3,0,1:T(8,128)(2,1)}, u32[]{:S(2)}, u32[]{:S(2)}) async-start(bf16[1,8,608,400]{2,3,0,1:T(8,128)(2,1)} %copy.37), calls=%async_computation.1 | async-start | bytes 8192000 | tf_op jit(solution)/shard_map/all_to_all | solution.py:78
  130.8 1.1 copy-start.1
  130.8 1.7 copy-start.3
  131.9 1.2 copy-start.5
  230.6 0.7 copy-start.7
Sparse Core Ops, SparseCore 0:
  48.8 63.6 all-gather.4
where the time goes:
time: 266 us; the launch traced here: 265 us
  waiting for transfers between devices  79.2 us (30%)
  local copies, waits for them, and re-layouts  75 us (28%)
  blocking collectives  67.1 us (25%)
  other arithmetic  14.9 us (6%)
  between operations  13.9 us (5%)
  matrix products  9.35 us (4%)
  starting transfers between devices  5.3 us (2%)
    all_to_all x1, waiting for transfers between devices, on_device(): lax.all_to_all(window_all, 'cohort', split_axis=1, concat_axis=0, tiled=T...  79.2 us
    gather x8, local copies, waits for them, and re-layouts, on_device(): jnp.take(expression, all_lists[source], axis=1)  46.6 us
    all_gather x2, blocking collectives, stacked_from(): parts = lax.all_gather(parts, axes[k])  27 us
    all_to_all x1, blocking collectives, summed_on_arrival(): lax.all_to_all(parts, axis, split_axis=0, concat_axis=0, tiled=True)  25.6 us
    all_to_all x1, blocking collectives, sent_to_all(): lax.all_to_all(jnp.broadcast_to(array[None], (peers, *array.shape)), axis...  14.6 us
    unnamed x17, local copies, waits for them, and re-layouts  9.05 us
    dot_general x1, matrix products, on_device(): jnp.einsum('cjs,cis->cji', column_all, window_part, preferred_element_typ...  8.76 us
    unnamed x7, other arithmetic  7.7 us
  transfers between devices with their start and end apart: 2, of which 1 were waited for; matrix products, arithmetic and copies ran while one was open for 22% of the time, Pallas kernels for 0%

commit v1 on v0

v1 whole, which is shorter than its diff:
```python
import functools

import jax
import jax.numpy as jnp
from jax import lax
from jax.experimental import pallas as pl
from jax.experimental.pallas import tpu as pltpu
from jax.sharding import Mesh
from jax.sharding import PartitionSpec as P

MODULES = 128
ROW_DEV = 152
COHORTS = 8
SAMPLES = 400
POOL = COHORTS * SAMPLES
GENES = 750
ROWS = 19
LANES = 128
TILES = POOL // LANES
DEPTH = 512
PITCH = POOL + 4
GENE_BLOCKS = 6
COHORT_AXES = ("z_lo", "core")
GENE_AXES = ("x", "y", "z_hi")
ALL_AXES = COHORT_AXES + GENE_AXES
UNROLL = 32
F32 = jnp.float32
BF16 = jnp.bfloat16


def transpose_in(load, blocks, turned):
    def column(k, _):
        lane = pl.multiple_of(k * LANES, LANES)
        for b in range(blocks):
            tile = load(b, lane)
            turned[pl.ds(b * PITCH + lane, LANES), :] = tile.T
        return _

    lax.fori_loop(0, TILES, column, 0)


def gather_rows(order, turned, grouped, blocks):
    def some(i, _):
        first = i * UNROLL
        for u in range(UNROLL):
            sample = order[first + u]
            grouped[pl.ds(first + u, blocks, stride=PITCH), :] = turned[
                pl.ds(sample, blocks, stride=PITCH), :
            ]
        return _

    lax.fori_loop(0, POOL // UNROLL, some, 0)


def standardized(grouped, cohort, block):
    x = grouped[pl.ds(block * PITCH + cohort * SAMPLES, SAMPLES), :]
    centred = x - jnp.sum(x, axis=0, keepdims=True) * (1.0 / SAMPLES)
    spread = jnp.sqrt(jnp.sum(centred * centred, axis=0, keepdims=True) + 0.01 * SAMPLES)
    return centred * (1.0 / spread)


def gene_kernel(order, x_ref, z_ref, turned, grouped):
    def load(b, lane):
        rows = min(LANES, GENES - b * LANES)
        tile = x_ref[b * LANES : b * LANES + rows, pl.ds(lane, LANES)].astype(F32)
        if rows < LANES:
            tile = jnp.concatenate([tile, jnp.zeros((LANES - rows, LANES), F32)], axis=0)
        return tile

    transpose_in(load, GENE_BLOCKS, turned)
    gather_rows(order, turned, grouped, GENE_BLOCKS)

    def cohort(c, _):
        for b in range(GENE_BLOCKS):
            z = standardized(grouped, c, b)
            z = jnp.concatenate([z, jnp.zeros((DEPTH - SAMPLES, LANES), F32)], axis=0)
            z_ref[c, b * LANES : (b + 1) * LANES, :] = z.T.astype(BF16)
        return _

    lax.fori_loop(0, COHORTS, cohort, 0)


def genes(order, x):
    return pl.pallas_call(
        gene_kernel,
        out_shape=jax.ShapeDtypeStruct((COHORTS, GENE_BLOCKS * LANES, DEPTH), BF16),
        in_specs=[
            pl.BlockSpec(memory_space=pltpu.SMEM),
            pl.BlockSpec(memory_space=pltpu.VMEM),
        ],
        out_specs=pl.BlockSpec(memory_space=pltpu.VMEM),
        scratch_shapes=[
            pltpu.VMEM((GENE_BLOCKS * PITCH, LANES), F32),
            pltpu.VMEM((GENE_BLOCKS * PITCH, LANES), F32),
        ],
        compiler_params=pltpu.CompilerParams(vmem_limit_bytes=56 * 2**20),
        name="genes",
    )(order, x)


def window_kernel(units, rows, order, place, module_ref, z_ref, *refs):
    parts, (out_ref, turned, grouped, zw, low, consensus) = refs[:units], refs[units:]
    total = sum(len_of(p) for p in parts) * rows
    blocks = total // LANES
    strips = [(p, j, r) for p in parts for j in range(p.shape[0]) for r in range(0, rows, 8)]

    def load(b, lane):
        return jnp.concatenate(
            [p[j, r : r + 8, pl.ds(lane, LANES)].astype(F32) for p, j, r in strips[b * 16 : (b + 1) * 16]],
            axis=0,
        )

    transpose_in(load, blocks, turned)
    gather_rows(order, turned, grouped, blocks)

    low[...] = jnp.full(low.shape, 2.0, F32)
    zw[SAMPLES:, :] = jnp.zeros((DEPTH - SAMPLES, total), BF16)

    def cohort(c, _):
        for b in range(blocks):
            zw[:SAMPLES, b * LANES : (b + 1) * LANES] = standardized(grouped, c, b).astype(BF16)
        corr = jnp.dot(z_ref[c], zw[...], preferred_element_type=F32)
        low[...] = jnp.minimum(low[...], corr)
        return _

    lax.fori_loop(0, COHORTS, cohort, 0)

    base = (1.0 + jnp.maximum(low[...], -1.0)) * 0.5
    square = base * base
    fourth = square * square
    consensus[...] = (fourth * fourth * fourth).astype(BF16)
    module = lax.broadcasted_iota(jnp.int32, (MODULES, GENE_BLOCKS * LANES), 0)
    onehot = jnp.where(module_ref[...] == module, 1.0, 0.0).astype(BF16)
    degree = jnp.dot(onehot, consensus[...], preferred_element_type=F32)
    turned_degree = degree.T
    for i in range(total // rows):
        at = pl.multiple_of(place[i] * rows, 8)
        out_ref[pl.ds(at, rows), :] = turned_degree[i * rows : (i + 1) * rows, :]


def len_of(ref):
    return ref.shape[0]


def windows(order, place, module, z, parts):
    rows = parts[0].shape[1]
    count = sum(p.shape[0] for p in parts)
    total = count * rows
    blocks = total // LANES
    return pl.pallas_call(
        functools.partial(window_kernel, len(parts), rows),
        out_shape=jax.ShapeDtypeStruct((total, MODULES), F32),
        in_specs=[
            pl.BlockSpec(memory_space=pltpu.SMEM),
            pl.BlockSpec(memory_space=pltpu.SMEM),
        ]
        + [pl.BlockSpec(memory_space=pltpu.VMEM)] * (2 + len(parts)),
        out_specs=pl.BlockSpec(memory_space=pltpu.VMEM),
        scratch_shapes=[
            pltpu.VMEM((blocks * PITCH, LANES), F32),
            pltpu.VMEM((blocks * PITCH, LANES), F32),
            pltpu.VMEM((DEPTH, total), BF16),
            pltpu.VMEM((GENE_BLOCKS * LANES, total), F32),
            pltpu.VMEM((GENE_BLOCKS * LANES, total), BF16),
        ],
        compiler_params=pltpu.CompilerParams(vmem_limit_bytes=56 * 2**20),
        name=f"windows_{total}",
    )(order, place, module, z, *parts)


def shifted(array, axis, by):
    n = lax.axis_size(axis)
    return lax.ppermute(array, axis, [(i, (i + by) % n) for i in range(n)])


def gathered(unit, first, second):
    line = [unit] + [shifted(unit, first, by) for by in (1, 3, 2)]
    stack = jnp.stack(line)
    ahead, behind = shifted(stack, second, 1), shifted(stack, second, 3)
    far = [shifted(ahead[:2], second, 1), shifted(behind[2:], second, 3)]
    parts = [stack, ahead, behind, *far]
    one = (0, -1, 1, 2)
    where = [(a, 0) for a in one] + [(a, -1) for a in one] + [(a, 1) for a in one] + [(a, 2) for a in one]
    return parts, where


def places(where, first, second):
    spots = []
    for a, b in where:
        at = {first: (lax.axis_index(first) + a) % 4, second: (lax.axis_index(second) + b) % 4}
        spots.append(at["x"] * 4 + at["y"])
    return jnp.stack(spots).astype(jnp.int32)


def on_device(expression, sample_index, gene_block):
    z_lo, core = lax.axis_index("z_lo"), lax.axis_index("core")
    share = z_lo * 2 + core
    mirror = (3 - z_lo) * 2 + core
    own = lax.dynamic_slice(expression, (share * ROWS, 0), (ROWS, POOL))
    theirs = lax.dynamic_slice(expression, (mirror * ROWS, 0), (ROWS, POOL))
    pairs = [(z * 2 + h, (3 - z) * 2 + 1 - h) for z in range(4) for h in range(2)]
    across = lax.ppermute(theirs, ("z_lo", "z_hi"), pairs)

    both = jnp.concatenate([sample_index, lax.ppermute(sample_index, "core", [(0, 1), (1, 0)])])
    order = jnp.concatenate([both] + [shifted(both, "z_lo", by) for by in (1, 2, 3)]).reshape(POOL)

    near, near_at = gathered(own[:16], "x", "y")
    rest = jnp.concatenate([own[16:], across, jnp.zeros((2, POOL), BF16)])
    z = genes(order, expression)
    module = jnp.pad(gene_block, (0, GENE_BLOCKS * LANES - GENES), constant_values=-1)[None]
    far, far_at = gathered(rest, "y", "x")

    low = windows(order, places(near_at, "x", "y"), module, z, near)
    high = windows(order, places(far_at, "y", "x"), module, z, far)

    parts = jnp.concatenate([low.reshape(16, 16, MODULES), high.reshape(16, 24, MODULES)], axis=1)
    arrived = lax.all_to_all(parts, ("x", "y"), 0, 0, tiled=True).sum(axis=0)
    mine, others = arrived[:ROWS], arrived[ROWS : 2 * ROWS]
    straight, crossed = [], []
    for c in range(COHORTS):
        for g in range(32):
            straight.append((c * 32 + g, g * 8 + c))
    for c in range(COHORTS):
        for g in range(32):
            crossed.append((c * 32 + g, (g ^ 1) * 8 + c))
    first = lax.ppermute(mine, ALL_AXES, straight)
    second = lax.ppermute(others, ALL_AXES, crossed)
    return jnp.log1p(first + second)


def solution(mesh):
    finer = Mesh(mesh.devices.reshape(4, 2, 4, 4, 2), ALL_AXES)
    placed = (P(GENE_AXES, None), P(COHORT_AXES, None), P(GENE_AXES))
    return jax.shard_map(
        on_device, mesh=finer, in_specs=placed, out_specs=P(ALL_AXES, None), check_vma=False
    )
```

time: 266 us -> 150 us (0.56)
  local copies, waits for them, and re-layouts: 75 us -> 8.96 us
  blocking collectives: 67.1 us -> 10.8 us
  Pallas kernels: 0 us -> 48.8 us
  waiting for transfers between devices: 79.2 us -> 36.7 us
  starting transfers between devices: 5.3 us -> 41.9 us
  between operations: 13.9 us -> 0.21 us
  other arithmetic: 14.9 us -> 1.94 us
  matrix products: 9.35 us -> 0 us
    all_to_all x1 -> x0, waiting for transfers between devices: 79.2 us -> none  [on_device(): lax.all_to_all(window_all, 'cohort', split_axis=1, concat_axis=0, tiled=T...]
    gather x9 -> x0, local copies, waits for them, and re-layouts: 52.1 us -> none  [the longest x8 46.6 us: on_device(): jnp.take(expression, all_lists[source], axis=1)]
    pallas_call x0 -> x3, Pallas kernels: none -> 48.8 us  [the longest x2 32.4 us: windows(): pl.pallas_call(functools.partial(window_kernel, len(parts), rows), out_sh...]
    ppermute x0 -> x21, starting transfers between devices: none -> 41.9 us  [the longest x17 22.8 us: shifted(): return lax.ppermute(array, axis, [(i, (i + by) % n) for i in range(n)])]
    ppermute x0 -> x21, waiting for transfers between devices: none -> 36.7 us  [the longest x17 22.2 us: shifted(): return lax.ppermute(array, axis, [(i, (i + by) % n) for i in range(n)])]
    all_to_all x2 -> x1, blocking collectives: 40.2 us -> 10.8 us  [on_device(): arrived = lax.all_to_all(parts, ('x', 'y'), 0, 0, tiled=True).sum(axis=0)]
    all_gather x2 -> x0, blocking collectives: 27 us -> none  [stacked_from(): parts = lax.all_gather(parts, axes[k])]
    dot_general x2 -> x0, matrix products: 9.35 us -> none  [the longest x1 8.76 us: on_device(): jnp.einsum('cjs,cis->cji', column_all, window_part, preferred_element_typ...]
  transfers between devices with their start and end apart: 2 -> 21, of which waited for: 1 -> 10; matrix products, arithmetic and copies ran while one was open for 22% -> 6% of each run, Pallas kernels for 0% -> 21%
where the time goes in v1:
time: 150 us; the launch traced here: 149 us
  Pallas kernels  48.8 us (33%)
  starting transfers between devices  41.9 us (28%)
  waiting for transfers between devices  36.7 us (24%)
  blocking collectives  10.8 us (7%)
  local copies, waits for them, and re-layouts  8.96 us (6%)
  other arithmetic  1.94 us (1%)
    pallas_call x2, Pallas kernels, windows(): pl.pallas_call(functools.partial(window_kernel, len(parts), rows), out_sh...  32.4 us
    ppermute x17, starting transfers between devices, shifted(): return lax.ppermute(array, axis, [(i, (i + by) % n) for i in range(n)])  22.8 us
    ppermute x17, waiting for transfers between devices, shifted(): return lax.ppermute(array, axis, [(i, (i + by) % n) for i in range(n)])  22.2 us
    pallas_call x1, Pallas kernels, genes(): pl.pallas_call(gene_kernel, out_shape=jax.ShapeDtypeStruct((COHORTS, GENE...  16.4 us
    all_to_all x1, blocking collectives, on_device(): arrived = lax.all_to_all(parts, ('x', 'y'), 0, 0, tiled=True).sum(axis=0)  10.8 us
    ppermute x1, starting transfers between devices, on_device(): first = lax.ppermute(mine, ALL_AXES, straight)  10.1 us
    ppermute x1, waiting for transfers between devices, on_device(): second = lax.ppermute(others, ALL_AXES, crossed)  8.34 us
    ppermute x1, starting transfers between devices, on_device(): across = lax.ppermute(theirs, ('z_lo', 'z_hi'), pairs)  5.66 us
  transfers between devices with their start and end apart: 21, of which 10 were waited for; matrix products, arithmetic and copies ran while one was open for 6% of the time, Pallas kernels for 21%

profile of v1, /device:TPU:1, one launch (start us, length us, event | category | flops | bytes accessed | tf_op | source)
XLA Modules:
  0.0 149.3 jit_solution(12507090936239598349)
XLA Ops:
  0.0 1.0 constant_dynamic-slice_fusion
  1.0 3.6 %collective-permute-start.6 = (bf16[16,3200]{1,0:T(8,128)(2,1)S(1)}, bf16[16,3200]{1,0:T(8,128)(2,1)S(1)}, u32[]{:S(2)}, u32[]{:S(2)}) collective-permute-start(bf16[16,3200]{1,0:T(8,128)(2,1)S(1)} %constant_dynamic-slice_fusion), channel_id=1, source_target_pairs={{0,16},{8,24},{16,0},{24,8},{1,17},{9,25},{17,1},{25,9},{2,18},{10... | collective-permute-start | bytes 307208 | tf_op jit(solution)/shard_map/ppermute | solution.py:173
  4.6 0.9 collective-permute-start.5
  5.5 1.0 constant_dynamic-slice_fusion.1
  6.5 5.7 %collective-permute-start.11 = (bf16[19,3200]{1,0:T(8,128)(2,1)S(1)}, bf16[19,3200]{1,0:T(8,128)(2,1)S(1)}, u32[]{:S(2)}, u32[]{:S(2)}) collective-permute-start(bf16[19,3200]{1,0:T(8,128)(2,1)S(1)} %constant_dynamic-slice_fusion.1), channel_id=1, source_target_pairs={{0,193},{1,192},{64,129},{65,128},{128,65},{129,64},{192,1},{193,0... | collective-permute-start | bytes 364808 | tf_op jit(solution)/shard_map/ppermute | solution.py:202
  12.1 0.9 fusion.1
  13.1 0.9 constant_dynamic-slice_fusion.2
  14.1 5.3 %collective-permute-done.11 = bf16[19,3200]{1,0:T(8,128)(2,1)S(1)} collective-permute-done((bf16[19,3200]{1,0:T(8,128)(2,1)S(1)}, bf16[19,3200]{1,0:T(8,128)(2,1)S(1)}, u32[]{:S(2)}, u32[]{:S(2)}) %collective-permute-start.11) | collective-permute-done | bytes 121632 | tf_op jit(solution)/shard_map/ppermute | solution.py:202
  19.5 3.0 %collective-permute-start.14 = (bf16[24,3200]{1,0:T(8,128)(2,1)S(1)}, bf16[24,3200]{1,0:T(8,128)(2,1)S(1)}, u32[]{:S(2)}, u32[]{:S(2)}) collective-permute-start(bf16[24,3200]{1,0:T(8,128)(2,1)S(1)} %maximum_maximum_fusion), channel_id=1, source_target_pairs={{0,4},{2,6},{4,0},{6,2},{1,5},{3,7},{5,1},{7,3},{8,12},{10,14},{12... | collective-permute-start | bytes 460808 | tf_op jit(solution)/shard_map/ppermute | solution.py:173
  22.5 0.8 collective-permute-start.13
  24.1 1.6 %collective-permute-done.14 = bf16[24,3200]{1,0:T(8,128)(2,1)S(1)} collective-permute-done((bf16[24,3200]{1,0:T(8,128)(2,1)S(1)}, bf16[24,3200]{1,0:T(8,128)(2,1)S(1)}, u32[]{:S(2)}, u32[]{:S(2)}) %collective-permute-start.14) | collective-permute-done | bytes 153632 | tf_op jit(solution)/shard_map/ppermute | solution.py:173
  26.3 3.2 %collective-permute-done.13 = bf16[24,3200]{1,0:T(8,128)(2,1)S(1)} collective-permute-done((bf16[24,3200]{1,0:T(8,128)(2,1)S(1)}, bf16[24,3200]{1,0:T(8,128)(2,1)S(1)}, u32[]{:S(2)}, u32[]{:S(2)}) %collective-permute-start.13) | collective-permute-done | bytes 153632 | tf_op jit(solution)/shard_map/ppermute | solution.py:173
  30.4 2.1 %collective-permute-start.16 = (bf16[4,24,3200]{2,1,0:T(8,128)(2,1)S(1)}, bf16[4,24,3200]{2,1,0:T(8,128)(2,1)S(1)}, u32[]{:S(2)}, u32[]{:S(2)}) collective-permute-start(bf16[4,24,3200]{2,1,0:T(8,128)(2,1)S(1)} %pad_maximum_fusion.refs_0_), channel_id=1, source_target_pairs={{0,24},{8,0},{16,8},{24,16},{1,25},{9,1},{17,9},{25,17},{2,26},{10... | collective-permute-start | bytes 1843208 | tf_op jit(solution)/shard_map/ppermute | solution.py:173
  32.5 2.0 %collective-permute-start.7 = (bf16[4,16,3200]{2,1,0:T(8,128)(2,1)S(1)}, bf16[4,16,3200]{2,1,0:T(8,128)(2,1)S(1)}, u32[]{:S(2)}, u32[]{:S(2)}) collective-permute-start(bf16[4,16,3200]{2,1,0:T(8,128)(2,1)S(1)} %pad_maximum_fusion.1.refs_0_), channel_id=1, source_target_pairs={{0,2},{2,4},{4,6},{6,0},{1,3},{3,5},{5,7},{7,1},{8,10},{10,12},{12... | collective-permute-start | bytes 1228808 | tf_op jit(solution)/shard_map/ppermute | solution.py:173
  34.6 1.5 collective-permute-start.8
  36.0 9.4 %collective-permute-done.15.refs_1_ = bf16[4,24,3200]{2,1,0:T(8,128)(2,1)S(1)} collective-permute-done((bf16[4,24,3200]{2,1,0:T(8,128)(2,1)S(1)}, bf16[4,24,3200]{2,1,0:T(8,128)(2,1)S(1)}, u32[]{:S(2)}, u32[]{:S(2)}) %collective-permute-start.15) | collective-permute-done | bytes 614432 | tf_op jit(solution)/shard_map/ppermute | solution.py:173
  45.6 0.9 slice.35
  46.4 2.6 %collective-permute-start.18 = (bf16[2,24,3200]{2,1,0:T(8,128)(2,1)}, bf16[2,24,3200]{2,1,0:T(8,128)(2,1)}, u32[]{:S(2)}, u32[]{:S(2)}) collective-permute-start(bf16[2,24,3200]{2,1,0:T(8,128)(2,1)} %slice.35), channel_id=1, source_target_pairs={{0,24},{8,0},{16,8},{24,16},{1,25},{9,1},{17,9},{25,17},{2,26},{10... | collective-permute-start | bytes 921608 | tf_op jit(solution)/shard_map/ppermute | solution.py:173
  49.8 2.3 %collective-permute-start.9 = (bf16[2,16,3200]{2,1,0:T(8,128)(2,1)}, bf16[2,16,3200]{2,1,0:T(8,128)(2,1)}, u32[]{:S(2)}, u32[]{:S(2)}) collective-permute-start(bf16[2,16,3200]{2,1,0:T(8,128)(2,1)} %slice.32), channel_id=1, source_target_pairs={{0,2},{2,4},{4,6},{6,0},{1,3},{3,5},{5,7},{7,1},{8,10},{10,12},{12... | collective-permute-start | bytes 614408 | tf_op jit(solution)/shard_map/ppermute | solution.py:173
  52.8 1.6 %collective-permute-start.10 = (bf16[2,16,3200]{2,1,0:T(8,128)(2,1)}, bf16[2,16,3200]{2,1,0:T(8,128)(2,1)}, u32[]{:S(2)}, u32[]{:S(2)}) collective-permute-start(bf16[2,16,3200]{2,1,0:T(8,128)(2,1)} %slice.33), channel_id=1, source_target_pairs={{0,6},{2,0},{4,2},{6,4},{1,7},{3,1},{5,3},{7,5},{8,14},{10,8},{12,... | collective-permute-start | bytes 614408 | tf_op jit(solution)/shard_map/ppermute | solution.py:173
  54.4 2.2 %collective-permute-start = (s32[1,400]{1,0:T(1,128)S(1)}, s32[1,400]{1,0:T(1,128)S(1)}, u32[]{:S(2)}, u32[]{:S(2)}) collective-permute-start(s32[1,400]{1,0:T(1,128)S(1)} %copy-done.7), channel_id=1, source_target_pairs={{0,32},{32,0},{1,33},{33,1},{2,34},{34,2},{3,35},{35,3},{4,36},{36... | collective-permute-start | bytes 4808 | tf_op jit(solution)/shard_map/ppermute | solution.py:204
  56.6 0.8 collective-permute-done
  57.7 4.2 %collective-permute-done.1 = s32[2,400]{1,0:T(2,128)S(1)} collective-permute-done((s32[2,400]{1,0:T(2,128)S(1)}, s32[2,400]{1,0:T(2,128)S(1)}, u32[]{:S(2)}, u32[]{:S(2)}) %collective-permute-start.1) | collective-permute-done | bytes 3232 | tf_op jit(solution)/shard_map/ppermute | solution.py:173
  61.9 3.4 %collective-permute-done.2 = s32[2,400]{1,0:T(2,128)S(1)} collective-permute-done((s32[2,400]{1,0:T(2,128)S(1)}, s32[2,400]{1,0:T(2,128)S(1)}, u32[]{:S(2)}, u32[]{:S(2)}) %collective-permute-start.2) | collective-permute-done | bytes 3232 | tf_op jit(solution)/shard_map/ppermute | solution.py:173
  68.5 16.4 %genes.1.z_ref = bf16[8,768,512]{2,1,0:T(8,128)(2,1)} custom-call(s32[3200]{0:T(1024)} %reshape.9.order, bf16[750,3200]{1,0:T(8,128)(2,1)} %x_ref.1), custom_call_target="tpu_custom_call" | custom-call | tf_op jit(solution)/shard_map/genes/pallas_call | solution.py:84
  84.9 14.9 %windows_256.1 = f32[256,128]{1,0:T(8,128)} custom-call(s32[3200]{0:T(1024)} %reshape.9.order, s32[16]{0:T(128)} %stack.116.place, s32[1,768]{1,0:T(1,128)} %broadcast_in_dim.6.module_ref, bf16[8,768,512]{2,1,0:T(8,128)(2,1)} %genes.1.z_ref, bf16[4,16,3200]{2,1,0:T(8,128)(2,1)} %copy-done.1, bf16[4,16,3200]{2,1,0:T(8,128)(2,1)} %copy-done.4, ...), custom_call_target="tpu_custom_call" | custom-call | tf_op jit(solution)/shard_map/windows_256/pallas_call | solution.py:150
  99.9 17.5 %windows_384.1 = f32[384,128]{1,0:T(8,128)} custom-call(s32[3200]{0:T(1024)} %reshape.9.order, s32[16]{0:T(128)} %stack.122.place, s32[1,768]{1,0:T(1,128)} %broadcast_in_dim.6.module_ref, bf16[8,768,512]{2,1,0:T(8,128)(2,1)} %genes.1.z_ref, bf16[4,24,3200]{2,1,0:T(8,128)(2,1)} %copy-done, bf16[4,24,3200]{2,1,0:T(8,128)(2,1)} %copy-done.2, ...), custom_call_target="tpu_custom_call" | custom-call | tf_op jit(solution)/shard_map/windows_384/pallas_call | solution.py:150
  117.3 0.9 pad_maximum_fusion.2
  118.3 10.8 %all_to_all.5 = f32[16,40,128]{2,1,0:T(8,128)S(1)} all-to-all(f32[16,40,128]{2,1,0:T(8,128)S(1)} %pad_maximum_fusion.2), channel_id=1, replica_groups=mesh['z_lo'=4,'core'=2,'x'=4,'y'=4,'z_hi'=2] {'x','y'}, dimensions={0} | all-to-all | bytes 655360 | tf_op jit(solution)/shard_map/all_to_all | solution.py:217
  129.1 10.1 %collective-permute-start.19 = (f32[19,128]{1,0:T(8,128)S(1)}, f32[19,128]{1,0:T(8,128)S(1)}, u32[]{:S(2)}, u32[]{:S(2)}) collective-permute-start(f32[19,128]{1,0:T(8,128)S(1)} %get-tuple-element.6), channel_id=1, source_target_pairs={{0,0},{1,8},{2,16},{3,24},{4,32},{5,40},{6,48},{7,56},{8,64},{9,72... | collective-permute-start | bytes 29192 | tf_op jit(solution)/shard_map/ppermute | solution.py:226
  139.2 1.2 collective-permute-start.20
  140.3 8.3 %collective-permute-done.20 = f32[19,128]{1,0:T(8,128)S(1)} collective-permute-done((f32[19,128]{1,0:T(8,128)S(1)}, f32[19,128]{1,0:T(8,128)S(1)}, u32[]{:S(2)}, u32[]{:S(2)}) %collective-permute-start.20) | collective-permute-done | bytes 9760 | tf_op jit(solution)/shard_map/ppermute | solution.py:227
  (57 shorter events, 8.2 us)
Async XLA Ops:
  0.0 54.4 %copy-start.7 = (s32[1,400]{1,0:T(1,128)S(1)}, s32[1,400]{1,0:T(1,128)}, u32[]{:S(2)}) copy-start(s32[1,400]{1,0:T(1,128)} %param.4) | copy-start | bytes 4804
  0.0 66.8 %copy-start.8 = (s32[750]{0:T(1024)S(1)}, s32[750]{0:T(1024)}, u32[]{:S(2)}) copy-start(s32[750]{0:T(1024)} %param.5) | copy-start | bytes 9004
  1.0 31.5 %collective-permute-start.6 = (bf16[16,3200]{1,0:T(8,128)(2,1)S(1)}, bf16[16,3200]{1,0:T(8,128)(2,1)S(1)}, u32[]{:S(2)}, u32[]{:S(2)}) collective-permute-start(bf16[16,3200]{1,0:T(8,128)(2,1)S(1)} %constant_dynamic-slice_fusion), channel_id=1, source_target_pairs={{0,16},{8,24},{16,0},{24,8},{1,17},{9,25},{17,1},{25,9},{2,18},{10... | collective-permute-start | bytes 307208 | tf_op jit(solution)/shard_map/ppermute | solution.py:173
  4.6 27.8 %collective-permute-start.5 = (bf16[16,3200]{1,0:T(8,128)(2,1)S(1)}, bf16[16,3200]{1,0:T(8,128)(2,1)S(1)}, u32[]{:S(2)}, u32[]{:S(2)}) collective-permute-start(bf16[16,3200]{1,0:T(8,128)(2,1)S(1)} %constant_dynamic-slice_fusion), channel_id=1, source_target_pairs={{0,24},{8,0},{16,8},{24,16},{1,25},{9,1},{17,9},{25,17},{2,26},{10... | collective-permute-start | bytes 307208 | tf_op jit(solution)/shard_map/ppermute | solution.py:173
  6.5 12.9 %collective-permute-start.11 = (bf16[19,3200]{1,0:T(8,128)(2,1)S(1)}, bf16[19,3200]{1,0:T(8,128)(2,1)S(1)}, u32[]{:S(2)}, u32[]{:S(2)}) collective-permute-start(bf16[19,3200]{1,0:T(8,128)(2,1)S(1)} %constant_dynamic-slice_fusion.1), channel_id=1, source_target_pairs={{0,193},{1,192},{64,129},{65,128},{128,65},{129,64},{192,1},{193,0... | collective-permute-start | bytes 364808 | tf_op jit(solution)/shard_map/ppermute | solution.py:202
  19.5 6.2 %collective-permute-start.14 = (bf16[24,3200]{1,0:T(8,128)(2,1)S(1)}, bf16[24,3200]{1,0:T(8,128)(2,1)S(1)}, u32[]{:S(2)}, u32[]{:S(2)}) collective-permute-start(bf16[24,3200]{1,0:T(8,128)(2,1)S(1)} %maximum_maximum_fusion), channel_id=1, source_target_pairs={{0,4},{2,6},{4,0},{6,2},{1,5},{3,7},{5,1},{7,3},{8,12},{10,14},{12... | collective-permute-start | bytes 460808 | tf_op jit(solution)/shard_map/ppermute | solution.py:173
  22.5 7.0 %collective-permute-start.13 = (bf16[24,3200]{1,0:T(8,128)(2,1)S(1)}, bf16[24,3200]{1,0:T(8,128)(2,1)S(1)}, u32[]{:S(2)}, u32[]{:S(2)}) collective-permute-start(bf16[24,3200]{1,0:T(8,128)(2,1)S(1)} %maximum_maximum_fusion), channel_id=1, source_target_pairs={{0,6},{2,0},{4,2},{6,4},{1,7},{3,1},{5,3},{7,5},{8,14},{10,8},{12,... | collective-permute-start | bytes 460808 | tf_op jit(solution)/shard_map/ppermute | solution.py:173
  23.3 6.3 %collective-permute-start.12 = (bf16[24,3200]{1,0:T(8,128)(2,1)S(1)}, bf16[24,3200]{1,0:T(8,128)(2,1)S(1)}, u32[]{:S(2)}, u32[]{:S(2)}) collective-permute-start(bf16[24,3200]{1,0:T(8,128)(2,1)S(1)} %maximum_maximum_fusion), channel_id=1, source_target_pairs={{0,2},{2,4},{4,6},{6,0},{1,3},{3,5},{5,7},{7,1},{8,10},{10,12},{12... | collective-permute-start | bytes 460808 | tf_op jit(solution)/shard_map/ppermute | solution.py:173
  25.7 6.8 %collective-permute-start.4 = (bf16[16,3200]{1,0:T(8,128)(2,1)S(1)}, bf16[16,3200]{1,0:T(8,128)(2,1)S(1)}, u32[]{:S(2)}, u32[]{:S(2)}) collective-permute-start(bf16[16,3200]{1,0:T(8,128)(2,1)S(1)} %constant_dynamic-slice_fusion), channel_id=1, source_target_pairs={{0,8},{8,16},{16,24},{24,0},{1,9},{9,17},{17,25},{25,1},{2,10},{10... | collective-permute-start | bytes 307208 | tf_op jit(solution)/shard_map/ppermute | solution.py:173
  29.7 55.2 %copy-start = (bf16[4,24,3200]{2,1,0:T(8,128)(2,1)}, bf16[4,24,3200]{2,1,0:T(8,128)(2,1)S(1)}, u32[]{:S(2)}) copy-start(bf16[4,24,3200]{2,1,0:T(8,128)(2,1)S(1)} %pad_maximum_fusion.refs_0_) | copy-start | bytes 1843204
  29.7 15.7 %collective-permute-start.15 = (bf16[4,24,3200]{2,1,0:T(8,128)(2,1)S(1)}, bf16[4,24,3200]{2,1,0:T(8,128)(2,1)S(1)}, u32[]{:S(2)}, u32[]{:S(2)}) collective-permute-start(bf16[4,24,3200]{2,1,0:T(8,128)(2,1)S(1)} %pad_maximum_fusion.refs_0_), channel_id=1, source_target_pairs={{0,8},{8,16},{16,24},{24,0},{1,9},{9,17},{17,25},{25,1},{2,10},{10... | collective-permute-start | bytes 1843208 | tf_op jit(solution)/shard_map/ppermute | solution.py:173
  30.4 15.2 %collective-permute-start.16 = (bf16[4,24,3200]{2,1,0:T(8,128)(2,1)S(1)}, bf16[4,24,3200]{2,1,0:T(8,128)(2,1)S(1)}, u32[]{:S(2)}, u32[]{:S(2)}) collective-permute-start(bf16[4,24,3200]{2,1,0:T(8,128)(2,1)S(1)} %pad_maximum_fusion.refs_0_), channel_id=1, source_target_pairs={{0,24},{8,0},{16,8},{24,16},{1,25},{9,1},{17,9},{25,17},{2,26},{10... | collective-permute-start | bytes 1843208 | tf_op jit(solution)/shard_map/ppermute | solution.py:173
  32.5 52.4 %copy-start.1 = (bf16[4,16,3200]{2,1,0:T(8,128)(2,1)}, bf16[4,16,3200]{2,1,0:T(8,128)(2,1)S(1)}, u32[]{:S(2)}) copy-start(bf16[4,16,3200]{2,1,0:T(8,128)(2,1)S(1)} %pad_maximum_fusion.1.refs_0_) | copy-start | bytes 1228804
  32.5 16.5 %collective-permute-start.7 = (bf16[4,16,3200]{2,1,0:T(8,128)(2,1)S(1)}, bf16[4,16,3200]{2,1,0:T(8,128)(2,1)S(1)}, u32[]{:S(2)}, u32[]{:S(2)}) collective-permute-start(bf16[4,16,3200]{2,1,0:T(8,128)(2,1)S(1)} %pad_maximum_fusion.1.refs_0_), channel_id=1, source_target_pairs={{0,2},{2,4},{4,6},{6,0},{1,3},{3,5},{5,7},{7,1},{8,10},{10,12},{12... | collective-permute-start | bytes 1228808 | tf_op jit(solution)/shard_map/ppermute | solution.py:173
  34.6 17.5 %collective-permute-start.8 = (bf16[4,16,3200]{2,1,0:T(8,128)(2,1)S(1)}, bf16[4,16,3200]{2,1,0:T(8,128)(2,1)S(1)}, u32[]{:S(2)}, u32[]{:S(2)}) collective-permute-start(bf16[4,16,3200]{2,1,0:T(8,128)(2,1)S(1)} %pad_maximum_fusion.1.refs_0_), channel_id=1, source_target_pairs={{0,6},{2,0},{4,2},{6,4},{1,7},{3,1},{5,3},{7,5},{8,14},{10,8},{12,... | collective-permute-start | bytes 1228808 | tf_op jit(solution)/shard_map/ppermute | solution.py:173
  45.4 39.5 %copy-start.2 = (bf16[4,24,3200]{2,1,0:T(8,128)(2,1)}, bf16[4,24,3200]{2,1,0:T(8,128)(2,1)S(1)}, u32[]{:S(2)}) copy-start(bf16[4,24,3200]{2,1,0:T(8,128)(2,1)S(1)} %collective-permute-done.15.refs_1_) | copy-start | bytes 1843204
  45.5 54.4 %collective-permute-start.17 = (bf16[2,24,3200]{2,1,0:T(8,128)(2,1)S(1)}, bf16[2,24,3200]{2,1,0:T(8,128)(2,1)}, u32[]{:S(2)}, u32[]{:S(2)}) collective-permute-start(bf16[2,24,3200]{2,1,0:T(8,128)(2,1)S(1)} %slice.34), channel_id=1, source_target_pairs={{0,8},{8,16},{16,24},{24,0},{1,9},{9,17},{17,25},{25,1},{2,10},{10... | collective-permute-start | bytes 921608 | tf_op jit(solution)/shard_map/ppermute | solution.py:173
  45.6 39.3 %copy-start.3 = (bf16[4,24,3200]{2,1,0:T(8,128)(2,1)}, bf16[4,24,3200]{2,1,0:T(8,128)(2,1)S(1)}, u32[]{:S(2)}) copy-start(bf16[4,24,3200]{2,1,0:T(8,128)(2,1)S(1)} %collective-permute-done.16.refs_2_) | copy-start | bytes 1843204
  46.4 53.4 %collective-permute-start.18 = (bf16[2,24,3200]{2,1,0:T(8,128)(2,1)}, bf16[2,24,3200]{2,1,0:T(8,128)(2,1)}, u32[]{:S(2)}, u32[]{:S(2)}) collective-permute-start(bf16[2,24,3200]{2,1,0:T(8,128)(2,1)} %slice.35), channel_id=1, source_target_pairs={{0,24},{8,0},{16,8},{24,16},{1,25},{9,1},{17,9},{25,17},{2,26},{10... | collective-permute-start | bytes 921608 | tf_op jit(solution)/shard_map/ppermute | solution.py:173
  49.0 35.9 %copy-start.4 = (bf16[4,16,3200]{2,1,0:T(8,128)(2,1)}, bf16[4,16,3200]{2,1,0:T(8,128)(2,1)S(1)}, u32[]{:S(2)}) copy-start(bf16[4,16,3200]{2,1,0:T(8,128)(2,1)S(1)} %collective-permute-done.7.refs_1_) | copy-start | bytes 1228804
  49.8 35.2 %collective-permute-start.9 = (bf16[2,16,3200]{2,1,0:T(8,128)(2,1)}, bf16[2,16,3200]{2,1,0:T(8,128)(2,1)}, u32[]{:S(2)}, u32[]{:S(2)}) collective-permute-start(bf16[2,16,3200]{2,1,0:T(8,128)(2,1)} %slice.32), channel_id=1, source_target_pairs={{0,2},{2,4},{4,6},{6,0},{1,3},{3,5},{5,7},{7,1},{8,10},{10,12},{12... | collective-permute-start | bytes 614408 | tf_op jit(solution)/shard_map/ppermute | solution.py:173
  52.1 32.9 %copy-start.5 = (bf16[4,16,3200]{2,1,0:T(8,128)(2,1)}, bf16[4,16,3200]{2,1,0:T(8,128)(2,1)S(1)}, u32[]{:S(2)}) copy-start(bf16[4,16,3200]{2,1,0:T(8,128)(2,1)S(1)} %collective-permute-done.8.refs_2_) | copy-start | bytes 1228804
  52.8 32.1 %collective-permute-start.10 = (bf16[2,16,3200]{2,1,0:T(8,128)(2,1)}, bf16[2,16,3200]{2,1,0:T(8,128)(2,1)}, u32[]{:S(2)}, u32[]{:S(2)}) collective-permute-start(bf16[2,16,3200]{2,1,0:T(8,128)(2,1)} %slice.33), channel_id=1, source_target_pairs={{0,6},{2,0},{4,2},{6,4},{1,7},{3,1},{5,3},{7,5},{8,14},{10,8},{12,... | collective-permute-start | bytes 614408 | tf_op jit(solution)/shard_map/ppermute | solution.py:173
  54.4 3.0 %collective-permute-start = (s32[1,400]{1,0:T(1,128)S(1)}, s32[1,400]{1,0:T(1,128)S(1)}, u32[]{:S(2)}, u32[]{:S(2)}) collective-permute-start(s32[1,400]{1,0:T(1,128)S(1)} %copy-done.7), channel_id=1, source_target_pairs={{0,32},{32,0},{1,33},{33,1},{2,34},{34,2},{3,35},{35,3},{4,36},{36... | collective-permute-start | bytes 4808 | tf_op jit(solution)/shard_map/ppermute | solution.py:204
  57.4 4.5 %collective-permute-start.1 = (s32[2,400]{1,0:T(2,128)S(1)}, s32[2,400]{1,0:T(2,128)S(1)}, u32[]{:S(2)}, u32[]{:S(2)}) collective-permute-start(s32[2,400]{1,0:T(2,128)S(1)} %pad_add_fusion), channel_id=1, source_target_pairs={{0,64},{64,128},{128,192},{192,0},{1,65},{65,129},{129,193},{193,1... | collective-permute-start | bytes 9608 | tf_op jit(solution)/shard_map/ppermute | solution.py:173
  61.9 3.4 %collective-permute-start.2 = (s32[2,400]{1,0:T(2,128)S(1)}, s32[2,400]{1,0:T(2,128)S(1)}, u32[]{:S(2)}, u32[]{:S(2)}) collective-permute-start(s32[2,400]{1,0:T(2,128)S(1)} %pad_add_fusion), channel_id=1, source_target_pairs={{0,128},{64,192},{128,0},{192,64},{1,129},{65,193},{129,1},{193,65... | collective-permute-start | bytes 9608 | tf_op jit(solution)/shard_map/ppermute | solution.py:173
  65.3 2.5 %collective-permute-start.3 = (s32[2,400]{1,0:T(2,128)S(1)}, s32[2,400]{1,0:T(2,128)S(1)}, u32[]{:S(2)}, u32[]{:S(2)}) collective-permute-start(s32[2,400]{1,0:T(2,128)S(1)} %pad_add_fusion), channel_id=1, source_target_pairs={{0,192},{64,0},{128,64},{192,128},{1,193},{65,1},{129,65},{193,129... | collective-permute-start | bytes 9608 | tf_op jit(solution)/shard_map/ppermute | solution.py:173
  99.8 17.5 %copy-start.6 = (f32[256,128]{1,0:T(8,128)S(1)}, f32[256,128]{1,0:T(8,128)}, u32[]{:S(2)}) copy-start(f32[256,128]{1,0:T(8,128)} %windows_256.1) | copy-start | bytes 393220
  129.1 11.2 %collective-permute-start.19 = (f32[19,128]{1,0:T(8,128)S(1)}, f32[19,128]{1,0:T(8,128)S(1)}, u32[]{:S(2)}, u32[]{:S(2)}) collective-permute-start(f32[19,128]{1,0:T(8,128)S(1)} %get-tuple-element.6), channel_id=1, source_target_pairs={{0,0},{1,8},{2,16},{3,24},{4,32},{5,40},{6,48},{7,56},{8,64},{9,72... | collective-permute-start | bytes 29192 | tf_op jit(solution)/shard_map/ppermute | solution.py:226
  139.2 9.5 %collective-permute-start.20 = (f32[19,128]{1,0:T(8,128)S(1)}, f32[19,128]{1,0:T(8,128)S(1)}, u32[]{:S(2)}, u32[]{:S(2)}) collective-permute-start(f32[19,128]{1,0:T(8,128)S(1)} %get-tuple-element.5), channel_id=1, source_target_pairs={{0,8},{1,0},{2,24},{3,16},{4,40},{5,32},{6,56},{7,48},{8,72},{9,64... | collective-permute-start | bytes 29192 | tf_op jit(solution)/shard_map/ppermute | solution.py:227

commit v2 on v1

v2 whole, which is shorter than its diff:
```python
import functools

import jax
import jax.numpy as jnp
from jax import lax
from jax.experimental import pallas as pl
from jax.experimental.pallas import tpu as pltpu
from jax.sharding import Mesh
from jax.sharding import PartitionSpec as P


MODULES = 128
COHORTS = 8
SAMPLES = 400
POOL = COHORTS * SAMPLES
GENES = 750
ROWS = 19
LANES = 128
TILES = POOL // LANES
DEPTH = 512
PITCH = POOL + 4
SHORT = SAMPLES + 4
CHUNK = 640
GENE_BLOCKS = 6
HALF = 3
COHORT_AXES = ("z_lo", "core")
GENE_AXES = ("x", "y", "z_hi")
ALL_AXES = COHORT_AXES + GENE_AXES
F32 = jnp.float32
BF16 = jnp.bfloat16


def transpose_in(load, blocks, turned, start, count):
    for k in range(start, start + count):
        for b in range(blocks):
            turned[b * PITCH + k * LANES : b * PITCH + (k + 1) * LANES, :] = load(b, k * LANES).T


def gather_cohort(order, cohort, turned, grouped, blocks):
    for u in range(SAMPLES):
        sample = order[cohort, u]
        grouped[pl.ds(u, blocks, stride=SHORT), :] = turned[pl.ds(sample, blocks, stride=PITCH), :]


def in_turn(order, turned, groups, blocks, finish):
    gather_cohort(order, 0, turned, groups[0], blocks)
    for c in range(COHORTS):
        if c + 1 < COHORTS:
            gather_cohort(order, c + 1, turned, groups[(c + 1) % 2], blocks)
        finish(c, c % 2)


def standardized(grouped, block):
    x = grouped[block * SHORT : block * SHORT + SAMPLES, :]
    centred = x - jnp.sum(x, axis=0, keepdims=True) * (1.0 / SAMPLES)
    spread = jnp.sqrt(jnp.sum(centred * centred, axis=0, keepdims=True) + 0.01 * SAMPLES)
    return centred * (1.0 / spread)


def gene_kernel(first, order, x_ref, z_ref, turned, even, odd):
    here = min(HALF * LANES, GENES - first * LANES)
    step = pl.program_id(0)

    for k in range(CHUNK // LANES):
        lane = pl.multiple_of(step * CHUNK, LANES) + k * LANES
        for b in range(HALF):
            rows = min(LANES, here - b * LANES)
            tile = x_ref[b * LANES : b * LANES + rows, k * LANES : (k + 1) * LANES].astype(F32)
            if rows < LANES:
                tile = jnp.concatenate([tile, jnp.zeros((LANES - rows, LANES), F32)], axis=0)
            turned[pl.ds(b * PITCH + lane, LANES), :] = tile.T

    def finish(c, slot):
        for b in range(HALF):
            z = standardized((even, odd)[slot], b)
            z = jnp.concatenate([z, jnp.zeros((DEPTH - SAMPLES, LANES), F32)], axis=0).astype(BF16)
            z_ref[c, b * LANES : (b + 1) * LANES, :] = z.T

    @pl.when(step == POOL // CHUNK - 1)
    def _():
        in_turn(order, turned, (even, odd), HALF, finish)


def genes(first, order, x):
    return pl.pallas_call(
        functools.partial(gene_kernel, first),
        grid=(POOL // CHUNK,),
        out_shape=jax.ShapeDtypeStruct((COHORTS, HALF * LANES, DEPTH), BF16),
        in_specs=[
            pl.BlockSpec(memory_space=pltpu.SMEM),
            pl.BlockSpec((HALF * LANES, CHUNK), lambda i: (first // HALF, i)),
        ],
        out_specs=pl.BlockSpec(memory_space=pltpu.VMEM),
        scratch_shapes=[
            pltpu.VMEM((HALF * PITCH, LANES), F32),
            pltpu.VMEM((HALF * SHORT, LANES), F32),
            pltpu.VMEM((HALF * SHORT, LANES), F32),
        ],
        compiler_params=pltpu.CompilerParams(vmem_limit_bytes=14 * 2**20),
    )(order, x)


def window_kernel(units, rows, order, place, module_ref, z_top, z_bottom, *refs):
    parts = refs[:units]
    out_ref, turned, even, odd, zw0, zw1, low, consensus = refs[units:]
    total = sum(p.shape[0] for p in parts) * rows
    blocks = total // LANES
    strips = [(p, j, r) for p in parts for j in range(p.shape[0]) for r in range(0, rows, 8)]

    def load(b, lane):
        return jnp.concatenate(
            [p[j, r : r + 8, lane : lane + LANES].astype(F32) for p, j, r in strips[b * 16 : (b + 1) * 16]],
            axis=0,
        )

    transpose_in(load, blocks, turned, 0, TILES)
    for zw in (zw0, zw1):
        zw[SAMPLES:, :] = jnp.zeros((DEPTH - SAMPLES, total), BF16)

    def finish(c, slot):
        zw = (zw0, zw1)[slot]
        for b in range(blocks):
            zw[:SAMPLES, b * LANES : (b + 1) * LANES] = standardized((even, odd)[slot], b).astype(BF16)
        for i, z_ref in enumerate((z_top, z_bottom)):
            half = slice(i * HALF * LANES, (i + 1) * HALF * LANES)
            corr = jnp.dot(z_ref[c], zw[...], preferred_element_type=F32)
            low[half, :] = jnp.minimum(low[half, :], corr) if c else corr

    in_turn(order, turned, (even, odd), blocks, finish)

    base = (1.0 + jnp.maximum(low[...], -1.0)) * 0.5
    square = base * base
    fourth = square * square
    consensus[...] = (fourth * fourth * fourth).astype(BF16)
    module = lax.broadcasted_iota(jnp.int32, (MODULES, GENE_BLOCKS * LANES), 0)
    onehot = jnp.where(module_ref[...] == module, 1.0, 0.0).astype(BF16)
    degree = jnp.dot(onehot, consensus[...], preferred_element_type=F32)
    turned_degree = degree.T
    for i in range(total // rows):
        at = pl.multiple_of(place[i] * rows, 8)
        out_ref[pl.ds(at, rows), :] = turned_degree[i * rows : (i + 1) * rows, :]


def windows(order, place, module, z, parts):
    rows = parts[0].shape[1]
    total = sum(p.shape[0] for p in parts) * rows
    blocks = total // LANES
    return pl.pallas_call(
        functools.partial(window_kernel, len(parts), rows),
        out_shape=jax.ShapeDtypeStruct((total, MODULES), F32),
        in_specs=[pl.BlockSpec(memory_space=pltpu.SMEM)] * 2
        + [pl.BlockSpec(memory_space=pltpu.VMEM)] * (3 + len(parts)),
        out_specs=pl.BlockSpec(memory_space=pltpu.VMEM),
        scratch_shapes=[
            pltpu.VMEM((blocks * PITCH, LANES), F32),
            pltpu.VMEM((blocks * SHORT, LANES), F32),
            pltpu.VMEM((blocks * SHORT, LANES), F32),
            pltpu.VMEM((DEPTH, total), BF16),
            pltpu.VMEM((DEPTH, total), BF16),
            pltpu.VMEM((GENE_BLOCKS * LANES, total), F32),
            pltpu.VMEM((GENE_BLOCKS * LANES, total), BF16),
        ],
        compiler_params=pltpu.CompilerParams(vmem_limit_bytes=20 * 2**20),
    )(order, place, module, *z, *parts)


def shifted(array, axis, by):
    n = lax.axis_size(axis)
    return lax.ppermute(array, axis, [(i, (i + by) % n) for i in range(n)])


def gathered(unit, first, second):
    line = [unit] + [shifted(unit, first, by) for by in (1, 3, 2)]
    stack = jnp.stack(line)
    ahead, behind = shifted(stack, second, 1), shifted(stack, second, 3)
    far = [shifted(ahead[:2], second, 1), shifted(behind[2:], second, 3)]
    parts = [stack, ahead, behind, *far]
    one = (0, -1, 1, 2)
    return parts, [(a, b) for b, many in ((0, one), (-1, one), (1, one), (2, one)) for a in many]


def places(where, first, second):
    spots = []
    for a, b in where:
        at = {first: (lax.axis_index(first) + a) % 4, second: (lax.axis_index(second) + b) % 4}
        spots.append(at["x"] * 4 + at["y"])
    return jnp.stack(spots).astype(jnp.int32)


def in_plane(expression, sample_index, gene_block):
    z_lo, core = lax.axis_index("z_lo"), lax.axis_index("core")
    share = z_lo * 2 + core
    mirror = (3 - z_lo) * 2 + core
    both = jnp.concatenate([sample_index, lax.ppermute(sample_index, "core", [(0, 1), (1, 0)])])
    theirs = lax.dynamic_slice(expression, (mirror * ROWS, 0), (ROWS, POOL))
    own = lax.dynamic_slice(expression, (share * ROWS, 0), (ROWS, POOL))
    pairs = [(z * 2 + h, (3 - z) * 2 + 1 - h) for z in range(4) for h in range(2)]
    across = lax.ppermute(theirs, ("z_lo", "z_hi"), pairs)
    order = jnp.concatenate([both] + [shifted(both, "z_lo", by) for by in (1, 2, 3)])

    near, near_at = gathered(own[:16], "x", "y")
    rest = jnp.concatenate([own[16:], across, jnp.zeros((2, POOL), BF16)])
    far, far_at = gathered(rest, "y", "x")
    z = [genes(0, order, expression), genes(HALF, order, expression)]
    module = jnp.pad(gene_block, (0, GENE_BLOCKS * LANES - GENES), constant_values=-1)[None]

    low = windows(order, places(near_at, "x", "y"), module, z, near)
    high = windows(order, places(far_at, "y", "x"), module, z, far)

    parts = jnp.concatenate([low.reshape(16, 16, MODULES), high.reshape(16, 24, MODULES)], axis=1)
    arrived = lax.all_to_all(parts, ("x", "y"), 0, 0, tiled=True).sum(axis=0)
    mine, others = arrived[:ROWS], arrived[ROWS : 2 * ROWS]
    straight, crossed = [], []
    for c in range(COHORTS):
        for g in range(32):
            straight.append((c * 32 + g, g * 8 + c))
    for c in range(COHORTS):
        for g in range(32):
            crossed.append((c * 32 + g, (g ^ 1) * 8 + c))
    first = lax.ppermute(mine, ALL_AXES, straight)
    second = lax.ppermute(others, ALL_AXES, crossed)
    return jnp.log1p(first + second)


def solution(mesh):
    finer = Mesh(mesh.devices.reshape(4, 2, 4, 4, 2), ALL_AXES)
    placed = (P(GENE_AXES, None), P(COHORT_AXES, None), P(GENE_AXES))
    return jax.shard_map(
        in_plane, mesh=finer, in_specs=placed, out_specs=P(ALL_AXES, None), check_vma=False
    )
```

time: 150 us -> 128 us (0.85)
  Pallas kernels: 48.8 us -> 26 us
  waiting for transfers between devices: 36.7 us -> 39 us
    pallas_call x2, Pallas kernels: 32.4 us -> 14.2 us  [windows(): pl.pallas_call(functools.partial(window_kernel, len(parts), rows), out_sh...]
    pallas_call x1 -> x2, Pallas kernels: 16.4 us -> 11.8 us  [genes(): pl.pallas_call(functools.partial(gene_kernel, first), grid=(POOL // CHUNK...]
    unnamed x18 -> x6, local copies, waits for them, and re-layouts: 0.03 us -> 2.36 us
    ppermute x17, waiting for transfers between devices: 22.2 us -> 24 us  [shifted(): return lax.ppermute(array, axis, [(i, (i + by) % n) for i in range(n)])]
  transfers between devices with their start and end apart: 21 -> 21, of which waited for: 10 -> 11; matrix products, arithmetic and copies ran while one was open for 6% -> 5% of each run, Pallas kernels for 21% -> 14%
where the time goes in v2:
time: 128 us
  starting transfers between devices  41.4 us (32%)
  waiting for transfers between devices  39 us (30%)
  Pallas kernels  26 us (20%)
  blocking collectives  10.8 us (8%)
  local copies, waits for them, and re-layouts  9.33 us (7%)
    ppermute x17, waiting for transfers between devices, shifted(): return lax.ppermute(array, axis, [(i, (i + by) % n) for i in range(n)])  24 us
    ppermute x17, starting transfers between devices, shifted(): return lax.ppermute(array, axis, [(i, (i + by) % n) for i in range(n)])  22.8 us
    pallas_call x2, Pallas kernels, windows(): pl.pallas_call(functools.partial(window_kernel, len(parts), rows), out_sh...  14.2 us
    pallas_call x2, Pallas kernels, genes(): pl.pallas_call(functools.partial(gene_kernel, first), grid=(POOL // CHUNK...  11.8 us
    all_to_all x1, blocking collectives, in_plane(): arrived = lax.all_to_all(parts, ('x', 'y'), 0, 0, tiled=True).sum(axis=0)  10.8 us
    ppermute x1, starting transfers between devices, in_plane(): first = lax.ppermute(mine, ALL_AXES, straight)  10.1 us
    ppermute x1, waiting for transfers between devices, in_plane(): second = lax.ppermute(others, ALL_AXES, crossed)  8.7 us
    ppermute x1, starting transfers between devices, in_plane(): across = lax.ppermute(theirs, ('z_lo', 'z_hi'), pairs)  5.66 us
  transfers between devices with their start and end apart: 21, of which 11 were waited for; matrix products, arithmetic and copies ran while one was open for 5% of the time, Pallas kernels for 14%

profile of v2, /device:TPU:1, one launch (start us, length us, event | category | flops | bytes accessed | tf_op | source)
XLA Modules:
  0.0 127.7 jit_solution(10526210033020801159)
XLA Ops:
  0.0 1.0 constant_dynamic-slice_fusion
  1.0 3.6 %collective-permute-start.6 = (bf16[16,3200]{1,0:T(8,128)(2,1)S(1)}, bf16[16,3200]{1,0:T(8,128)(2,1)S(1)}, u32[]{:S(2)}, u32[]{:S(2)}) collective-permute-start(bf16[16,3200]{1,0:T(8,128)(2,1)S(1)} %constant_dynamic-slice_fusion), channel_id=1, source_target_pairs={{0,16},{8,24},{16,0},{24,8},{1,17},{9,25},{17,1},{25,9},{2,18},{10... | collective-permute-start | bytes 307208 | tf_op jit(solution)/shard_map/ppermute | solution.py:169
  4.6 0.9 collective-permute-start.5
  5.5 1.0 constant_dynamic-slice_fusion.1
  6.5 5.7 %collective-permute-start.11 = (bf16[19,3200]{1,0:T(8,128)(2,1)S(1)}, bf16[19,3200]{1,0:T(8,128)(2,1)S(1)}, u32[]{:S(2)}, u32[]{:S(2)}) collective-permute-start(bf16[19,3200]{1,0:T(8,128)(2,1)S(1)} %constant_dynamic-slice_fusion.1), channel_id=1, source_target_pairs={{0,193},{1,192},{64,129},{65,128},{128,65},{129,64},{192,1},{193,0... | collective-permute-start | bytes 364808 | tf_op jit(solution)/shard_map/ppermute | solution.py:198
  12.1 0.9 fusion.1
  13.1 0.9 constant_dynamic-slice_fusion.2
  14.1 5.3 %collective-permute-done.11 = bf16[19,3200]{1,0:T(8,128)(2,1)S(1)} collective-permute-done((bf16[19,3200]{1,0:T(8,128)(2,1)S(1)}, bf16[19,3200]{1,0:T(8,128)(2,1)S(1)}, u32[]{:S(2)}, u32[]{:S(2)}) %collective-permute-start.11) | collective-permute-done | bytes 121632 | tf_op jit(solution)/shard_map/ppermute | solution.py:198
  19.5 3.0 %collective-permute-start.14 = (bf16[24,3200]{1,0:T(8,128)(2,1)S(1)}, bf16[24,3200]{1,0:T(8,128)(2,1)S(1)}, u32[]{:S(2)}, u32[]{:S(2)}) collective-permute-start(bf16[24,3200]{1,0:T(8,128)(2,1)S(1)} %maximum_maximum_fusion), channel_id=1, source_target_pairs={{0,4},{2,6},{4,0},{6,2},{1,5},{3,7},{5,1},{7,3},{8,12},{10,14},{12... | collective-permute-start | bytes 460808 | tf_op jit(solution)/shard_map/ppermute | solution.py:169
  22.5 0.8 collective-permute-start.13
  24.1 1.6 %collective-permute-done.14 = bf16[24,3200]{1,0:T(8,128)(2,1)S(1)} collective-permute-done((bf16[24,3200]{1,0:T(8,128)(2,1)S(1)}, bf16[24,3200]{1,0:T(8,128)(2,1)S(1)}, u32[]{:S(2)}, u32[]{:S(2)}) %collective-permute-start.14) | collective-permute-done | bytes 153632 | tf_op jit(solution)/shard_map/ppermute | solution.py:169
  26.3 3.2 %collective-permute-done.13 = bf16[24,3200]{1,0:T(8,128)(2,1)S(1)} collective-permute-done((bf16[24,3200]{1,0:T(8,128)(2,1)S(1)}, bf16[24,3200]{1,0:T(8,128)(2,1)S(1)}, u32[]{:S(2)}, u32[]{:S(2)}) %collective-permute-start.13) | collective-permute-done | bytes 153632 | tf_op jit(solution)/shard_map/ppermute | solution.py:169
  30.4 2.1 %collective-permute-start.16 = (bf16[4,24,3200]{2,1,0:T(8,128)(2,1)S(1)}, bf16[4,24,3200]{2,1,0:T(8,128)(2,1)S(1)}, u32[]{:S(2)}, u32[]{:S(2)}) collective-permute-start(bf16[4,24,3200]{2,1,0:T(8,128)(2,1)S(1)} %pad_maximum_fusion.refs_0_), channel_id=1, source_target_pairs={{0,24},{8,0},{16,8},{24,16},{1,25},{9,1},{17,9},{25,17},{2,26},{10... | collective-permute-start | bytes 1843208 | tf_op jit(solution)/shard_map/ppermute | solution.py:169
  32.5 2.0 %collective-permute-start.7 = (bf16[4,16,3200]{2,1,0:T(8,128)(2,1)S(1)}, bf16[4,16,3200]{2,1,0:T(8,128)(2,1)S(1)}, u32[]{:S(2)}, u32[]{:S(2)}) collective-permute-start(bf16[4,16,3200]{2,1,0:T(8,128)(2,1)S(1)} %pad_maximum_fusion.1.refs_0_), channel_id=1, source_target_pairs={{0,2},{2,4},{4,6},{6,0},{1,3},{3,5},{5,7},{7,1},{8,10},{10,12},{12... | collective-permute-start | bytes 1228808 | tf_op jit(solution)/shard_map/ppermute | solution.py:169
  34.5 1.5 %collective-permute-start.8 = (bf16[4,16,3200]{2,1,0:T(8,128)(2,1)S(1)}, bf16[4,16,3200]{2,1,0:T(8,128)(2,1)S(1)}, u32[]{:S(2)}, u32[]{:S(2)}) collective-permute-start(bf16[4,16,3200]{2,1,0:T(8,128)(2,1)S(1)} %pad_maximum_fusion.1.refs_0_), channel_id=1, source_target_pairs={{0,6},{2,0},{4,2},{6,4},{1,7},{3,1},{5,3},{7,5},{8,14},{10,8},{12,... | collective-permute-start | bytes 1228808 | tf_op jit(solution)/shard_map/ppermute | solution.py:169
  36.0 9.4 %collective-permute-done.15.refs_1_ = bf16[4,24,3200]{2,1,0:T(8,128)(2,1)S(1)} collective-permute-done((bf16[4,24,3200]{2,1,0:T(8,128)(2,1)S(1)}, bf16[4,24,3200]{2,1,0:T(8,128)(2,1)S(1)}, u32[]{:S(2)}, u32[]{:S(2)}) %collective-permute-start.15) | collective-permute-done | bytes 614432 | tf_op jit(solution)/shard_map/ppermute | solution.py:169
  46.9 2.7 %collective-permute-start.18 = (bf16[2,24,3200]{2,1,0:T(8,128)(2,1)}, bf16[2,24,3200]{2,1,0:T(8,128)(2,1)}, u32[]{:S(2)}, u32[]{:S(2)}) collective-permute-start(bf16[2,24,3200]{2,1,0:T(8,128)(2,1)} %slice.35), channel_id=1, source_target_pairs={{0,24},{8,0},{16,8},{24,16},{1,25},{9,1},{17,9},{25,17},{2,26},{10... | collective-permute-start | bytes 921608 | tf_op jit(solution)/shard_map/ppermute | solution.py:169
  50.3 2.3 %collective-permute-start.9 = (bf16[2,16,3200]{2,1,0:T(8,128)(2,1)}, bf16[2,16,3200]{2,1,0:T(8,128)(2,1)}, u32[]{:S(2)}, u32[]{:S(2)}) collective-permute-start(bf16[2,16,3200]{2,1,0:T(8,128)(2,1)} %slice.32), channel_id=1, source_target_pairs={{0,2},{2,4},{4,6},{6,0},{1,3},{3,5},{5,7},{7,1},{8,10},{10,12},{12... | collective-permute-start | bytes 614408 | tf_op jit(solution)/shard_map/ppermute | solution.py:169
  53.3 1.6 %collective-permute-start.10 = (bf16[2,16,3200]{2,1,0:T(8,128)(2,1)}, bf16[2,16,3200]{2,1,0:T(8,128)(2,1)}, u32[]{:S(2)}, u32[]{:S(2)}) collective-permute-start(bf16[2,16,3200]{2,1,0:T(8,128)(2,1)} %slice.33), channel_id=1, source_target_pairs={{0,6},{2,0},{4,2},{6,4},{1,7},{3,1},{5,3},{7,5},{8,14},{10,8},{12,... | collective-permute-start | bytes 614408 | tf_op jit(solution)/shard_map/ppermute | solution.py:169
  54.8 2.2 %collective-permute-start = (s32[1,400]{1,0:T(1,128)S(1)}, s32[1,400]{1,0:T(1,128)S(1)}, u32[]{:S(2)}, u32[]{:S(2)}) collective-permute-start(s32[1,400]{1,0:T(1,128)S(1)} %copy-done.1), channel_id=1, source_target_pairs={{0,32},{32,0},{1,33},{33,1},{2,34},{34,2},{3,35},{35,3},{4,36},{36... | collective-permute-start | bytes 4808 | tf_op jit(solution)/shard_map/ppermute | solution.py:194
  57.0 0.8 collective-permute-done
  58.1 4.2 %collective-permute-done.1 = s32[2,400]{1,0:T(2,128)S(1)} collective-permute-done((s32[2,400]{1,0:T(2,128)S(1)}, s32[2,400]{1,0:T(2,128)S(1)}, u32[]{:S(2)}, u32[]{:S(2)}) %collective-permute-start.1) | collective-permute-done | bytes 3232 | tf_op jit(solution)/shard_map/ppermute | solution.py:169
  62.4 3.4 %collective-permute-done.2 = s32[2,400]{1,0:T(2,128)S(1)} collective-permute-done((s32[2,400]{1,0:T(2,128)S(1)}, s32[2,400]{1,0:T(2,128)S(1)}, u32[]{:S(2)}, u32[]{:S(2)}) %collective-permute-start.2) | collective-permute-done | bytes 3232 | tf_op jit(solution)/shard_map/ppermute | solution.py:169
  66.2 2.0 %collective-permute-done.3 = s32[2,400]{1,0:T(2,128)S(1)} collective-permute-done((s32[2,400]{1,0:T(2,128)S(1)}, s32[2,400]{1,0:T(2,128)S(1)}, u32[]{:S(2)}, u32[]{:S(2)}) %collective-permute-start.3) | collective-permute-done | bytes 3232 | tf_op jit(solution)/shard_map/ppermute | solution.py:169
  68.2 2.4 %copy-done = bf16[750,3200]{1,0:T(8,128)(2,1)S(1)} copy-done((bf16[750,3200]{1,0:T(8,128)(2,1)S(1)}, bf16[750,3200]{1,0:T(8,128)(2,1)}, u32[]{:S(2)}) %copy-start) | copy-done | bytes 4800024
  70.6 5.8 %shard_map.37.z_top = bf16[8,384,512]{2,1,0:T(8,128)(2,1)S(1)} custom-call(s32[8,400]{1,0:T(8,128)S(1)} %concatenate.14.order, bf16[750,3200]{1,0:T(8,128)(2,1)S(1)} %copy-done), custom_call_target="tpu_custom_call" | custom-call | tf_op jit(solution)/shard_map/pallas_call | solution.py:85
  76.4 6.0 %shard_map.38.z_bottom = bf16[8,384,512]{2,1,0:T(8,128)(2,1)S(1)} custom-call(s32[8,400]{1,0:T(8,128)S(1)} %concatenate.14.order, bf16[750,3200]{1,0:T(8,128)(2,1)S(1)} %copy-done), custom_call_target="tpu_custom_call" | custom-call | tf_op jit(solution)/shard_map/pallas_call | solution.py:85
  82.4 6.4 %shard_map.39 = f32[256,128]{1,0:T(8,128)S(1)} custom-call(s32[8,400]{1,0:T(8,128)S(1)} %concatenate.14.order, s32[16]{0:T(128)S(1)} %stack.116.place, s32[1,768]{1,0:T(1,128)S(1)} %broadcast_in_dim.6.module_ref, bf16[8,384,512]{2,1,0:T(8,128)(2,1)S(1)} %shard_map.37.z_top, bf16[8,384,512]{2,1,0:T(8,128)(2,1)S(1)} %shard_map.38.z_bottom, ...), custom_call_target="tpu_custom_call" | custom-call | tf_op jit(solution)/shard_map/pallas_call | solution.py:148
  88.8 7.8 %shard_map.40 = f32[384,128]{1,0:T(8,128)S(1)} custom-call(s32[8,400]{1,0:T(8,128)S(1)} %concatenate.14.order, s32[16]{0:T(128)S(1)} %stack.122.place, s32[1,768]{1,0:T(1,128)S(1)} %broadcast_in_dim.6.module_ref, bf16[8,384,512]{2,1,0:T(8,128)(2,1)S(1)} %shard_map.37.z_top, bf16[8,384,512]{2,1,0:T(8,128)(2,1)S(1)} %shard_map.38.z_bottom, ...), custom_call_target="tpu_custom_call" | custom-call | tf_op jit(solution)/shard_map/pallas_call | solution.py:148
  96.7 10.8 %all_to_all.5 = f32[16,40,128]{2,1,0:T(8,128)S(1)} all-to-all(f32[16,40,128]{2,1,0:T(8,128)S(1)} %pad_maximum_fusion.2), channel_id=1, replica_groups=mesh['z_lo'=4,'core'=2,'x'=4,'y'=4,'z_hi'=2] {'x','y'}, dimensions={0} | all-to-all | bytes 655360 | tf_op jit(solution)/shard_map/all_to_all | solution.py:211
  107.5 10.1 %collective-permute-start.19 = (f32[19,128]{1,0:T(8,128)S(1)}, f32[19,128]{1,0:T(8,128)S(1)}, u32[]{:S(2)}, u32[]{:S(2)}) collective-permute-start(f32[19,128]{1,0:T(8,128)S(1)} %get-tuple-element.6), channel_id=1, source_target_pairs={{0,0},{1,8},{2,16},{3,24},{4,32},{5,40},{6,48},{7,56},{8,64},{9,72... | collective-permute-start | bytes 29192 | tf_op jit(solution)/shard_map/ppermute | solution.py:220
  118.4 8.7 %collective-permute-done.20 = f32[19,128]{1,0:T(8,128)S(1)} collective-permute-done((f32[19,128]{1,0:T(8,128)S(1)}, f32[19,128]{1,0:T(8,128)S(1)}, u32[]{:S(2)}, u32[]{:S(2)}) %collective-permute-start.20) | collective-permute-done | bytes 9760 | tf_op jit(solution)/shard_map/ppermute | solution.py:221
  (45 shorter events, 7.6 us)
Async XLA Ops:
  0.0 54.8 %copy-start.1 = (s32[1,400]{1,0:T(1,128)S(1)}, s32[1,400]{1,0:T(1,128)}, u32[]{:S(2)}) copy-start(s32[1,400]{1,0:T(1,128)} %param.4) | copy-start | bytes 4804
  0.0 66.2 %copy-start.2 = (s32[750]{0:T(1024)S(1)}, s32[750]{0:T(1024)}, u32[]{:S(2)}) copy-start(s32[750]{0:T(1024)} %param.5) | copy-start | bytes 9004
  1.0 31.5 %collective-permute-start.6 = (bf16[16,3200]{1,0:T(8,128)(2,1)S(1)}, bf16[16,3200]{1,0:T(8,128)(2,1)S(1)}, u32[]{:S(2)}, u32[]{:S(2)}) collective-permute-start(bf16[16,3200]{1,0:T(8,128)(2,1)S(1)} %constant_dynamic-slice_fusion), channel_id=1, source_target_pairs={{0,16},{8,24},{16,0},{24,8},{1,17},{9,25},{17,1},{25,9},{2,18},{10... | collective-permute-start | bytes 307208 | tf_op jit(solution)/shard_map/ppermute | solution.py:169
  4.6 27.8 %collective-permute-start.5 = (bf16[16,3200]{1,0:T(8,128)(2,1)S(1)}, bf16[16,3200]{1,0:T(8,128)(2,1)S(1)}, u32[]{:S(2)}, u32[]{:S(2)}) collective-permute-start(bf16[16,3200]{1,0:T(8,128)(2,1)S(1)} %constant_dynamic-slice_fusion), channel_id=1, source_target_pairs={{0,24},{8,0},{16,8},{24,16},{1,25},{9,1},{17,9},{25,17},{2,26},{10... | collective-permute-start | bytes 307208 | tf_op jit(solution)/shard_map/ppermute | solution.py:169
  6.5 12.9 %collective-permute-start.11 = (bf16[19,3200]{1,0:T(8,128)(2,1)S(1)}, bf16[19,3200]{1,0:T(8,128)(2,1)S(1)}, u32[]{:S(2)}, u32[]{:S(2)}) collective-permute-start(bf16[19,3200]{1,0:T(8,128)(2,1)S(1)} %constant_dynamic-slice_fusion.1), channel_id=1, source_target_pairs={{0,193},{1,192},{64,129},{65,128},{128,65},{129,64},{192,1},{193,0... | collective-permute-start | bytes 364808 | tf_op jit(solution)/shard_map/ppermute | solution.py:198
  19.5 6.2 %collective-permute-start.14 = (bf16[24,3200]{1,0:T(8,128)(2,1)S(1)}, bf16[24,3200]{1,0:T(8,128)(2,1)S(1)}, u32[]{:S(2)}, u32[]{:S(2)}) collective-permute-start(bf16[24,3200]{1,0:T(8,128)(2,1)S(1)} %maximum_maximum_fusion), channel_id=1, source_target_pairs={{0,4},{2,6},{4,0},{6,2},{1,5},{3,7},{5,1},{7,3},{8,12},{10,14},{12... | collective-permute-start | bytes 460808 | tf_op jit(solution)/shard_map/ppermute | solution.py:169
  22.5 7.0 %collective-permute-start.13 = (bf16[24,3200]{1,0:T(8,128)(2,1)S(1)}, bf16[24,3200]{1,0:T(8,128)(2,1)S(1)}, u32[]{:S(2)}, u32[]{:S(2)}) collective-permute-start(bf16[24,3200]{1,0:T(8,128)(2,1)S(1)} %maximum_maximum_fusion), channel_id=1, source_target_pairs={{0,6},{2,0},{4,2},{6,4},{1,7},{3,1},{5,3},{7,5},{8,14},{10,8},{12,... | collective-permute-start | bytes 460808 | tf_op jit(solution)/shard_map/ppermute | solution.py:169
  23.3 6.3 %collective-permute-start.12 = (bf16[24,3200]{1,0:T(8,128)(2,1)S(1)}, bf16[24,3200]{1,0:T(8,128)(2,1)S(1)}, u32[]{:S(2)}, u32[]{:S(2)}) collective-permute-start(bf16[24,3200]{1,0:T(8,128)(2,1)S(1)} %maximum_maximum_fusion), channel_id=1, source_target_pairs={{0,2},{2,4},{4,6},{6,0},{1,3},{3,5},{5,7},{7,1},{8,10},{10,12},{12... | collective-permute-start | bytes 460808 | tf_op jit(solution)/shard_map/ppermute | solution.py:169
  25.7 6.8 %collective-permute-start.4 = (bf16[16,3200]{1,0:T(8,128)(2,1)S(1)}, bf16[16,3200]{1,0:T(8,128)(2,1)S(1)}, u32[]{:S(2)}, u32[]{:S(2)}) collective-permute-start(bf16[16,3200]{1,0:T(8,128)(2,1)S(1)} %constant_dynamic-slice_fusion), channel_id=1, source_target_pairs={{0,8},{8,16},{16,24},{24,0},{1,9},{9,17},{17,25},{25,1},{2,10},{10... | collective-permute-start | bytes 307208 | tf_op jit(solution)/shard_map/ppermute | solution.py:169
  29.7 15.8 %collective-permute-start.15 = (bf16[4,24,3200]{2,1,0:T(8,128)(2,1)S(1)}, bf16[4,24,3200]{2,1,0:T(8,128)(2,1)S(1)}, u32[]{:S(2)}, u32[]{:S(2)}) collective-permute-start(bf16[4,24,3200]{2,1,0:T(8,128)(2,1)S(1)} %pad_maximum_fusion.refs_0_), channel_id=1, source_target_pairs={{0,8},{8,16},{16,24},{24,0},{1,9},{9,17},{17,25},{25,1},{2,10},{10... | collective-permute-start | bytes 1843208 | tf_op jit(solution)/shard_map/ppermute | solution.py:169
  30.4 15.8 %collective-permute-start.16 = (bf16[4,24,3200]{2,1,0:T(8,128)(2,1)S(1)}, bf16[4,24,3200]{2,1,0:T(8,128)(2,1)S(1)}, u32[]{:S(2)}, u32[]{:S(2)}) collective-permute-start(bf16[4,24,3200]{2,1,0:T(8,128)(2,1)S(1)} %pad_maximum_fusion.refs_0_), channel_id=1, source_target_pairs={{0,24},{8,0},{16,8},{24,16},{1,25},{9,1},{17,9},{25,17},{2,26},{10... | collective-permute-start | bytes 1843208 | tf_op jit(solution)/shard_map/ppermute | solution.py:169
  32.5 17.1 %collective-permute-start.7 = (bf16[4,16,3200]{2,1,0:T(8,128)(2,1)S(1)}, bf16[4,16,3200]{2,1,0:T(8,128)(2,1)S(1)}, u32[]{:S(2)}, u32[]{:S(2)}) collective-permute-start(bf16[4,16,3200]{2,1,0:T(8,128)(2,1)S(1)} %pad_maximum_fusion.1.refs_0_), channel_id=1, source_target_pairs={{0,2},{2,4},{4,6},{6,0},{1,3},{3,5},{5,7},{7,1},{8,10},{10,12},{12... | collective-permute-start | bytes 1228808 | tf_op jit(solution)/shard_map/ppermute | solution.py:169
  34.5 18.0 %collective-permute-start.8 = (bf16[4,16,3200]{2,1,0:T(8,128)(2,1)S(1)}, bf16[4,16,3200]{2,1,0:T(8,128)(2,1)S(1)}, u32[]{:S(2)}, u32[]{:S(2)}) collective-permute-start(bf16[4,16,3200]{2,1,0:T(8,128)(2,1)S(1)} %pad_maximum_fusion.1.refs_0_), channel_id=1, source_target_pairs={{0,6},{2,0},{4,2},{6,4},{1,7},{3,1},{5,3},{7,5},{8,14},{10,8},{12,... | collective-permute-start | bytes 1228808 | tf_op jit(solution)/shard_map/ppermute | solution.py:169
  46.2 42.6 %collective-permute-start.17 = (bf16[2,24,3200]{2,1,0:T(8,128)(2,1)}, bf16[2,24,3200]{2,1,0:T(8,128)(2,1)S(1)}, u32[]{:S(2)}, u32[]{:S(2)}) collective-permute-start(bf16[2,24,3200]{2,1,0:T(8,128)(2,1)} %slice.34), channel_id=1, source_target_pairs={{0,8},{8,16},{16,24},{24,0},{1,9},{9,17},{17,25},{25,1},{2,10},{10... | collective-permute-start | bytes 921608 | tf_op jit(solution)/shard_map/ppermute | solution.py:169
  46.9 41.9 %collective-permute-start.18 = (bf16[2,24,3200]{2,1,0:T(8,128)(2,1)}, bf16[2,24,3200]{2,1,0:T(8,128)(2,1)}, u32[]{:S(2)}, u32[]{:S(2)}) collective-permute-start(bf16[2,24,3200]{2,1,0:T(8,128)(2,1)} %slice.35), channel_id=1, source_target_pairs={{0,24},{8,0},{16,8},{24,16},{1,25},{9,1},{17,9},{25,17},{2,26},{10... | collective-permute-start | bytes 921608 | tf_op jit(solution)/shard_map/ppermute | solution.py:169
  50.3 32.1 %collective-permute-start.9 = (bf16[2,16,3200]{2,1,0:T(8,128)(2,1)}, bf16[2,16,3200]{2,1,0:T(8,128)(2,1)}, u32[]{:S(2)}, u32[]{:S(2)}) collective-permute-start(bf16[2,16,3200]{2,1,0:T(8,128)(2,1)} %slice.32), channel_id=1, source_target_pairs={{0,2},{2,4},{4,6},{6,0},{1,3},{3,5},{5,7},{7,1},{8,10},{10,12},{12... | collective-permute-start | bytes 614408 | tf_op jit(solution)/shard_map/ppermute | solution.py:169
  53.3 29.1 %collective-permute-start.10 = (bf16[2,16,3200]{2,1,0:T(8,128)(2,1)}, bf16[2,16,3200]{2,1,0:T(8,128)(2,1)}, u32[]{:S(2)}, u32[]{:S(2)}) collective-permute-start(bf16[2,16,3200]{2,1,0:T(8,128)(2,1)} %slice.33), channel_id=1, source_target_pairs={{0,6},{2,0},{4,2},{6,4},{1,7},{3,1},{5,3},{7,5},{8,14},{10,8},{12,... | collective-permute-start | bytes 614408 | tf_op jit(solution)/shard_map/ppermute | solution.py:169
  54.8 3.0 %collective-permute-start = (s32[1,400]{1,0:T(1,128)S(1)}, s32[1,400]{1,0:T(1,128)S(1)}, u32[]{:S(2)}, u32[]{:S(2)}) collective-permute-start(s32[1,400]{1,0:T(1,128)S(1)} %copy-done.1), channel_id=1, source_target_pairs={{0,32},{32,0},{1,33},{33,1},{2,34},{34,2},{3,35},{35,3},{4,36},{36... | collective-permute-start | bytes 4808 | tf_op jit(solution)/shard_map/ppermute | solution.py:194
  57.9 4.5 %collective-permute-start.1 = (s32[2,400]{1,0:T(2,128)S(1)}, s32[2,400]{1,0:T(2,128)S(1)}, u32[]{:S(2)}, u32[]{:S(2)}) collective-permute-start(s32[2,400]{1,0:T(2,128)S(1)} %pad_add_fusion), channel_id=1, source_target_pairs={{0,64},{64,128},{128,192},{192,0},{1,65},{65,129},{129,193},{193,1... | collective-permute-start | bytes 9608 | tf_op jit(solution)/shard_map/ppermute | solution.py:169
  62.4 3.4 %collective-permute-start.2 = (s32[2,400]{1,0:T(2,128)S(1)}, s32[2,400]{1,0:T(2,128)S(1)}, u32[]{:S(2)}, u32[]{:S(2)}) collective-permute-start(s32[2,400]{1,0:T(2,128)S(1)} %pad_add_fusion), channel_id=1, source_target_pairs={{0,128},{64,192},{128,0},{192,64},{1,129},{65,193},{129,1},{193,65... | collective-permute-start | bytes 9608 | tf_op jit(solution)/shard_map/ppermute | solution.py:169
  65.7 2.5 %collective-permute-start.3 = (s32[2,400]{1,0:T(2,128)S(1)}, s32[2,400]{1,0:T(2,128)S(1)}, u32[]{:S(2)}, u32[]{:S(2)}) collective-permute-start(s32[2,400]{1,0:T(2,128)S(1)} %pad_add_fusion), channel_id=1, source_target_pairs={{0,192},{64,0},{128,64},{192,128},{1,193},{65,1},{129,65},{193,129... | collective-permute-start | bytes 9608 | tf_op jit(solution)/shard_map/ppermute | solution.py:169
  68.2 2.4 %copy-start = (bf16[750,3200]{1,0:T(8,128)(2,1)S(1)}, bf16[750,3200]{1,0:T(8,128)(2,1)}, u32[]{:S(2)}) copy-start(bf16[750,3200]{1,0:T(8,128)(2,1)} %x_ref.3) | copy-start | bytes 14400004
  107.5 10.9 %collective-permute-start.19 = (f32[19,128]{1,0:T(8,128)S(1)}, f32[19,128]{1,0:T(8,128)S(1)}, u32[]{:S(2)}, u32[]{:S(2)}) collective-permute-start(f32[19,128]{1,0:T(8,128)S(1)} %get-tuple-element.6), channel_id=1, source_target_pairs={{0,0},{1,8},{2,16},{3,24},{4,32},{5,40},{6,48},{7,56},{8,64},{9,72... | collective-permute-start | bytes 29192 | tf_op jit(solution)/shard_map/ppermute | solution.py:220
  117.6 9.5 %collective-permute-start.20 = (f32[19,128]{1,0:T(8,128)S(1)}, f32[19,128]{1,0:T(8,128)S(1)}, u32[]{:S(2)}, u32[]{:S(2)}) collective-permute-start(f32[19,128]{1,0:T(8,128)S(1)} %get-tuple-element.5), channel_id=1, source_target_pairs={{0,8},{1,0},{2,24},{3,16},{4,40},{5,32},{6,56},{7,48},{8,72},{9,64... | collective-permute-start | bytes 29192 | tf_op jit(solution)/shard_map/ppermute | solution.py:221

commit v3 on v2

v3 whole, which is shorter than its diff:
```python
import functools

import jax
import jax.numpy as jnp
from jax import lax
from jax.experimental import pallas as pl
from jax.experimental.pallas import tpu as pltpu
from jax.sharding import Mesh
from jax.sharding import PartitionSpec as P


MODULES = 128
ROW_DEV = 152
COHORTS = 8
SAMPLES = 400
POOL = COHORTS * SAMPLES
GENES = 750
ROWS = 19
LANES = 128
TILES = POOL // LANES
DEPTH = 512
PITCH = POOL + 4
SHORT = SAMPLES + 4
CHUNK = 640
GENE_BLOCKS = 6
COHORT_AXES = ("z_lo", "core")
GENE_AXES = ("x", "y", "z_hi")
ALL_AXES = COHORT_AXES + GENE_AXES
F32 = jnp.float32
BF16 = jnp.bfloat16


def transpose_in(load, blocks, turned, start, count):
    for k in range(start, start + count):
        for b in range(blocks):
            turned[b * PITCH + k * LANES : b * PITCH + (k + 1) * LANES, :] = load(b, k * LANES).T


def gather_cohort(source, turned, grouped, blocks):
    for u in range(SAMPLES):
        sample = source[0][source[1], u]
        grouped[pl.ds(u, blocks, stride=SHORT), :] = turned[pl.ds(sample, blocks, stride=PITCH), :]


def in_turn(order, turned, groups, blocks, finish):
    gather_cohort(order[0], turned, groups[0], blocks)
    for c in range(COHORTS):
        if c + 1 < COHORTS:
            gather_cohort(order[c + 1], turned, groups[(c + 1) % 2], blocks)
        finish(c, c % 2)


def standardized(grouped, block):
    x = grouped[block * SHORT : block * SHORT + SAMPLES, :]
    centred = x - jnp.sum(x, axis=0, keepdims=True) * (1.0 / SAMPLES)
    spread = jnp.sqrt(jnp.sum(centred * centred, axis=0, keepdims=True) + 0.01 * SAMPLES)
    return centred * (1.0 / spread)


def order_of(refs):
    return [(ref, row) for ref in refs for row in range(2)]


def gene_kernel(*refs):
    lists, (x_hbm, z_ref, x_ref, turned, even, odd, arrive) = refs[:4], refs[4:]

    def fetch(i):
        lanes = pl.ds(pl.multiple_of(i * CHUNK, LANES), CHUNK)
        return pltpu.make_async_copy(x_hbm.at[:, lanes], x_ref.at[:, lanes], arrive.at[i])

    for i in range(POOL // CHUNK):
        fetch(i).start()

    def chunk(i, _):
        fetch(i).wait()
        for k in range(CHUNK // LANES):
            lane = pl.multiple_of(i * CHUNK, LANES) + k * LANES
            for b in range(GENE_BLOCKS):
                rows = min(LANES, GENES - b * LANES)
                tile = x_ref[b * LANES : b * LANES + rows, pl.ds(lane, LANES)].astype(F32)
                if rows < LANES:
                    tile = jnp.concatenate([tile, jnp.zeros((LANES - rows, LANES), F32)], axis=0)
                turned[pl.ds(b * PITCH + lane, LANES), :] = tile.T
        return _

    lax.fori_loop(0, POOL // CHUNK, chunk, 0)

    def finish(c, slot):
        for b in range(GENE_BLOCKS):
            z = standardized((even, odd)[slot], b)
            z = jnp.concatenate([z, jnp.zeros((DEPTH - SAMPLES, LANES), F32)], axis=0).astype(BF16)
            z_ref[c, b * LANES : (b + 1) * LANES, :] = z.T

    in_turn(order_of(lists), turned, (even, odd), GENE_BLOCKS, finish)


def genes(lists, x):
    return pl.pallas_call(
        gene_kernel,
        out_shape=jax.ShapeDtypeStruct((COHORTS, GENE_BLOCKS * LANES, DEPTH), BF16),
        in_specs=[pl.BlockSpec(memory_space=pltpu.SMEM)] * 4 + [pl.BlockSpec(memory_space=pltpu.HBM)],
        out_specs=pl.BlockSpec(memory_space=pltpu.VMEM),
        scratch_shapes=[
            pltpu.VMEM((GENES, POOL), BF16),
            pltpu.VMEM((GENE_BLOCKS * PITCH, LANES), F32),
            pltpu.VMEM((GENE_BLOCKS * SHORT, LANES), F32),
            pltpu.VMEM((GENE_BLOCKS * SHORT, LANES), F32),
            pltpu.SemaphoreType.DMA((POOL // CHUNK,)),
        ],
        compiler_params=pltpu.CompilerParams(vmem_limit_bytes=26 * 2**20),
        name="genes",
    )(*lists, x)


def pick_kernel(x_ref, near_ref, mine_ref, theirs_ref):
    z_lo, core = lax.axis_index("z_lo"), lax.axis_index("core")
    own = (z_lo * 2 + core) * ROWS
    other = ((3 - z_lo) * 2 + core) * ROWS
    row = lax.broadcasted_iota(jnp.int32, (64, ROW_DEV), 0)
    column = lax.broadcasted_iota(jnp.int32, (64, ROW_DEV), 1)
    wanted = jnp.where(
        row < 19, own + row, jnp.where((row >= 43) & (row < 62), other + row - 43, -1)
    )
    select = jnp.where(column == wanted, 1.0, 0.0).astype(BF16)
    rows = jnp.dot(select, x_ref[...], preferred_element_type=F32).astype(BF16)
    near_ref[...] = rows[:16]
    mine_ref[...] = rows[16:40]
    theirs_ref[...] = rows[40:]


def pick(x):
    return pl.pallas_call(
        pick_kernel,
        out_shape=[jax.ShapeDtypeStruct((rows, POOL), BF16) for rows in (16, 24, 24)],
        in_specs=[pl.BlockSpec(memory_space=pltpu.VMEM)],
        out_specs=[pl.BlockSpec(memory_space=pltpu.VMEM)] * 3,
        compiler_params=pltpu.CompilerParams(vmem_limit_bytes=6 * 2**20),
        name="pick",
    )(x)


def window_kernel(units, rows, axes, where, before, *refs):
    lists, (module_ref, z_ref), refs = refs[:4], refs[4:6], refs[6:]
    early, parts, refs = refs[:before], refs[before : before + units], refs[before + units :]
    out_ref, turned, even, odd, zw0, zw1, low, consensus, label = refs
    total = sum(p.shape[0] for p in parts) * rows
    blocks = total // LANES
    strips = [(p, j, r) for p in parts for j in range(p.shape[0]) for r in range(0, rows, 8)]

    def load(b, lane):
        return jnp.concatenate(
            [p[j, r : r + 8, lane : lane + LANES].astype(F32) for p, j, r in strips[b * 16 : (b + 1) * 16]],
            axis=0,
        )

    transpose_in(load, blocks, turned, 0, TILES)
    for zw in (zw0, zw1):
        zw[SAMPLES:, :] = jnp.zeros((DEPTH - SAMPLES, total), BF16)

    def finish(c, slot):
        zw = (zw0, zw1)[slot]
        for b in range(blocks):
            zw[:SAMPLES, b * LANES : (b + 1) * LANES] = standardized((even, odd)[slot], b).astype(BF16)
        corr = jnp.dot(z_ref[c], zw[...], preferred_element_type=F32)
        low[...] = jnp.minimum(low[...], corr) if c else corr

    in_turn(order_of(lists), turned, (even, odd), blocks, finish)

    base = (1.0 + jnp.maximum(low[...], -1.0)) * 0.5
    square = base * base
    fourth = square * square
    consensus[...] = (fourth * fourth * fourth).astype(BF16)
    label[...] = jnp.full(label.shape, -1, jnp.int32)
    label[:, :GENES] = module_ref[...]
    module = lax.broadcasted_iota(jnp.int32, (MODULES, GENE_BLOCKS * LANES), 0)
    onehot = jnp.where(label[...] == module, 1.0, 0.0).astype(BF16)
    degree = jnp.dot(onehot, consensus[...], preferred_element_type=F32).T
    first, second = (lax.axis_index(axis) for axis in axes)
    for i, (a, b) in enumerate(where):
        spot = {axes[0]: lax.rem(first + a + 4, 4), axes[1]: lax.rem(second + b + 4, 4)}
        out_ref[spot["x"] * 4 + spot["y"], before * 16 : before * 16 + rows, :] = degree[
            i * rows : (i + 1) * rows, :
        ]
    if before:
        out_ref[:, :16, :] = early[0][...]


def windows(lists, module, z, parts, axes, where, early=()):
    rows = parts[0].shape[1]
    total = sum(p.shape[0] for p in parts) * rows
    blocks = total // LANES
    return pl.pallas_call(
        functools.partial(window_kernel, len(parts), rows, axes, where, len(early)),
        out_shape=jax.ShapeDtypeStruct((16, rows + 16 * len(early), MODULES), F32),
        in_specs=[pl.BlockSpec(memory_space=pltpu.SMEM)] * 4
        + [pl.BlockSpec(memory_space=pltpu.VMEM)] * (2 + len(early) + len(parts)),
        out_specs=pl.BlockSpec(memory_space=pltpu.VMEM),
        scratch_shapes=[
            pltpu.VMEM((blocks * PITCH, LANES), F32),
            pltpu.VMEM((blocks * SHORT, LANES), F32),
            pltpu.VMEM((blocks * SHORT, LANES), F32),
            pltpu.VMEM((DEPTH, total), BF16),
            pltpu.VMEM((DEPTH, total), BF16),
            pltpu.VMEM((GENE_BLOCKS * LANES, total), F32),
            pltpu.VMEM((GENE_BLOCKS * LANES, total), BF16),
            pltpu.VMEM((1, GENE_BLOCKS * LANES), jnp.int32),
        ],
        compiler_params=pltpu.CompilerParams(vmem_limit_bytes=20 * 2**20),
    )(*lists, module, z, *early, *parts)


def shifted(array, axis, by):
    n = lax.axis_size(axis)
    return lax.ppermute(array, axis, [(i, (i + by) % n) for i in range(n)])


def gathered(unit, first, second):
    line = [unit] + [shifted(unit, first, by) for by in (1, 3, 2)]
    stack = jnp.stack(line)
    ahead, behind = shifted(stack, second, 1), shifted(stack, second, 3)
    far = [shifted(ahead[:2], second, 1), shifted(behind[2:], second, 3)]
    parts = [stack, ahead, behind, *far]
    one = (0, -1, 1, 2)
    return parts, [(a, b) for b, many in ((0, one), (-1, one), (1, one), (2, one)) for a in many]


def in_plane(expression, sample_index, gene_block):
    own, mine, theirs = pick(expression[:ROW_DEV])
    both = jnp.concatenate([sample_index, lax.ppermute(sample_index, "core", [(0, 1), (1, 0)])])
    pairs = [(z * 2 + h, (3 - z) * 2 + 1 - h) for z in range(4) for h in range(2)]
    across = lax.ppermute(theirs, ("z_lo", "z_hi"), pairs)
    lists = [both] + [shifted(both, "z_lo", by) for by in (1, 2, 3)]

    near, near_at = gathered(own, "x", "y")
    far, far_at = gathered(mine + across, "y", "x")
    z = genes(lists, expression)
    module = gene_block.reshape(1, GENES)

    low = windows(lists, module, z, near, ("x", "y"), near_at)
    parts = windows(lists, module, z, far, ("y", "x"), far_at, (low,))

    arrived = lax.all_to_all(parts, ("x", "y"), 0, 0, tiled=True).sum(axis=0)
    mine, others = arrived[:ROWS], arrived[ROWS : 2 * ROWS]
    straight, crossed = [], []
    for c in range(COHORTS):
        for g in range(32):
            straight.append((c * 32 + g, g * 8 + c))
    for c in range(COHORTS):
        for g in range(32):
            crossed.append((c * 32 + g, (g ^ 1) * 8 + c))
    first = lax.ppermute(mine, ALL_AXES, straight)
    second = lax.ppermute(others, ALL_AXES, crossed)
    return jnp.log1p(first + second)


def solution(mesh):
    finer = Mesh(mesh.devices.reshape(4, 2, 4, 4, 2), ALL_AXES)
    placed = (P(GENE_AXES, None), P(COHORT_AXES, None), P(GENE_AXES))
    return jax.shard_map(in_plane, mesh=finer, in_specs=placed, out_specs=P(ALL_AXES, None), check_vma=False)
```

time: 128 us -> 116 us (0.906)
  local copies, waits for them, and re-layouts: 9.33 us -> 1.51 us
  starting transfers between devices: 41.4 us -> 38 us
  Pallas kernels: 26 us -> 22.9 us
  waiting for transfers between devices: 39 us -> 40.5 us
    ppermute x17, starting transfers between devices: 22.8 us -> 17.9 us  [shifted(): return lax.ppermute(array, axis, [(i, (i + by) % n) for i in range(n)])]
    pallas_call x4, Pallas kernels: 26 us -> 22.9 us  [the longest x2 14.9 us: windows(): pl.pallas_call(functools.partial(window_kernel, len(parts), rows, axes, w...]
    slice x4, local copies, waits for them, and re-layouts: 2.85 us -> 0.07 us  [gathered(): far = [shifted(ahead[:2], second, 1), shifted(behind[2:], second, 3)]]
    unnamed x6, local copies, waits for them, and re-layouts: 2.36 us -> 0.01 us
    ppermute x1, waiting for transfers between devices: 5.32 us -> 7.28 us  [in_plane(): across = lax.ppermute(theirs, ('z_lo', 'z_hi'), pairs)]
  transfers between devices with their start and end apart: 21 -> 21, of which waited for: 11 -> 9; matrix products, arithmetic and copies ran while one was open for 5% -> 0% of each run, Pallas kernels for 14% -> 12%
where the time goes in v3:
time: 116 us
  waiting for transfers between devices  40.5 us (35%)
  starting transfers between devices  38 us (33%)
  Pallas kernels  22.9 us (20%)
  blocking collectives  11.8 us (10%)
  local copies, waits for them, and re-layouts  1.51 us (1%)
    ppermute x17, waiting for transfers between devices, shifted(): return lax.ppermute(array, axis, [(i, (i + by) % n) for i in range(n)])  23.6 us
    ppermute x17, starting transfers between devices, shifted(): return lax.ppermute(array, axis, [(i, (i + by) % n) for i in range(n)])  17.9 us
    pallas_call x2, Pallas kernels, windows(): pl.pallas_call(functools.partial(window_kernel, len(parts), rows, axes, w...  14.9 us
    all_to_all x1, blocking collectives, in_plane(): arrived = lax.all_to_all(parts, ('x', 'y'), 0, 0, tiled=True).sum(axis=0)  11.8 us
    ppermute x1, starting transfers between devices, in_plane(): first = lax.ppermute(mine, ALL_AXES, straight)  9.89 us
    ppermute x1, waiting for transfers between devices, in_plane(): second = lax.ppermute(others, ALL_AXES, crossed)  8.7 us
    pallas_call x1, Pallas kernels, genes(): pl.pallas_call(gene_kernel, out_shape=jax.ShapeDtypeStruct((COHORTS, GENE...  7.69 us
    ppermute x1, waiting for transfers between devices, in_plane(): across = lax.ppermute(theirs, ('z_lo', 'z_hi'), pairs)  7.28 us
  transfers between devices with their start and end apart: 21, of which 9 were waited for; matrix products, arithmetic and copies ran while one was open for 0% of the time, Pallas kernels for 12%

profile of v3, /device:TPU:1, one launch (start us, length us, event | category | flops | bytes accessed | tf_op | source)
XLA Modules:
  0.0 115.7 jit_solution(1352765678295679153)
XLA Ops:
  0.0 1.4 %slice.21.x_ref = bf16[152,3200]{1,0:T(8,128)(2,1)S(1)} slice(bf16[750,3200]{1,0:T(8,128)(2,1)} %refs_4_.1), slice={[0:152], [0:3200]} | slice | bytes 1945600 | tf_op jit(solution)/shard_map/slice | solution.py:228
  1.4 0.3 pick.1
  1.7 6.5 %collective-permute-start.11 = (bf16[24,3200]{1,0:T(8,128)(2,1)S(1)}, bf16[24,3200]{1,0:T(8,128)(2,1)S(1)}, u32[]{:S(2)}, u32[]{:S(2)}) collective-permute-start(bf16[24,3200]{1,0:T(8,128)(2,1)S(1)} %get-tuple-element.10), channel_id=1, source_target_pairs={{0,193},{1,192},{64,129},{65,128},{128,65},{129,64},{192,1},{193,0... | collective-permute-start | bytes 460808 | tf_op jit(solution)/shard_map/ppermute | solution.py:231
  8.2 7.3 %collective-permute-done.11 = bf16[24,3200]{1,0:T(8,128)(2,1)S(1)} collective-permute-done((bf16[24,3200]{1,0:T(8,128)(2,1)S(1)}, bf16[24,3200]{1,0:T(8,128)(2,1)S(1)}, u32[]{:S(2)}, u32[]{:S(2)}) %collective-permute-start.11) | collective-permute-done | bytes 153632 | tf_op jit(solution)/shard_map/ppermute | solution.py:231
  15.5 1.4 %collective-permute-start.12 = (bf16[24,3200]{1,0:T(8,128)(2,1)S(1)}, bf16[24,3200]{1,0:T(8,128)(2,1)S(1)}, u32[]{:S(2)}, u32[]{:S(2)}) collective-permute-start(bf16[24,3200]{1,0:T(8,128)(2,1)S(1)} %add.6), channel_id=1, source_target_pairs={{0,2},{2,4},{4,6},{6,0},{1,3},{3,5},{5,7},{7,1},{8,10},{10,12},{12... | collective-permute-start | bytes 460808 | tf_op jit(solution)/shard_map/ppermute | solution.py:214
  16.9 1.6 %collective-permute-start.13 = (bf16[24,3200]{1,0:T(8,128)(2,1)S(1)}, bf16[24,3200]{1,0:T(8,128)(2,1)S(1)}, u32[]{:S(2)}, u32[]{:S(2)}) collective-permute-start(bf16[24,3200]{1,0:T(8,128)(2,1)S(1)} %add.6), channel_id=1, source_target_pairs={{0,6},{2,0},{4,2},{6,4},{1,7},{3,1},{5,3},{7,5},{8,14},{10,8},{12,... | collective-permute-start | bytes 460808 | tf_op jit(solution)/shard_map/ppermute | solution.py:214
  18.5 1.6 %collective-permute-start.14 = (bf16[24,3200]{1,0:T(8,128)(2,1)S(1)}, bf16[24,3200]{1,0:T(8,128)(2,1)S(1)}, u32[]{:S(2)}, u32[]{:S(2)}) collective-permute-start(bf16[24,3200]{1,0:T(8,128)(2,1)S(1)} %add.6), channel_id=1, source_target_pairs={{0,4},{2,6},{4,0},{6,2},{1,5},{3,7},{5,1},{7,3},{8,12},{10,14},{12... | collective-permute-start | bytes 460808 | tf_op jit(solution)/shard_map/ppermute | solution.py:214
  20.0 1.2 %collective-permute-start.4 = (bf16[16,3200]{1,0:T(8,128)(2,1)S(1)}, bf16[16,3200]{1,0:T(8,128)(2,1)S(1)}, u32[]{:S(2)}, u32[]{:S(2)}) collective-permute-start(bf16[16,3200]{1,0:T(8,128)(2,1)S(1)} %get-tuple-element.8), channel_id=1, source_target_pairs={{0,8},{8,16},{16,24},{24,0},{1,9},{9,17},{17,25},{25,1},{2,10},{10... | collective-permute-start | bytes 307208 | tf_op jit(solution)/shard_map/ppermute | solution.py:214
  21.2 1.5 %collective-permute-start.5 = (bf16[16,3200]{1,0:T(8,128)(2,1)S(1)}, bf16[16,3200]{1,0:T(8,128)(2,1)S(1)}, u32[]{:S(2)}, u32[]{:S(2)}) collective-permute-start(bf16[16,3200]{1,0:T(8,128)(2,1)S(1)} %get-tuple-element.8), channel_id=1, source_target_pairs={{0,24},{8,0},{16,8},{24,16},{1,25},{9,1},{17,9},{25,17},{2,26},{10... | collective-permute-start | bytes 307208 | tf_op jit(solution)/shard_map/ppermute | solution.py:214
  22.7 1.6 %collective-permute-start.6 = (bf16[16,3200]{1,0:T(8,128)(2,1)S(1)}, bf16[16,3200]{1,0:T(8,128)(2,1)S(1)}, u32[]{:S(2)}, u32[]{:S(2)}) collective-permute-start(bf16[16,3200]{1,0:T(8,128)(2,1)S(1)} %get-tuple-element.8), channel_id=1, source_target_pairs={{0,16},{8,24},{16,0},{24,8},{1,17},{9,25},{17,1},{25,9},{2,18},{10... | collective-permute-start | bytes 307208 | tf_op jit(solution)/shard_map/ppermute | solution.py:214
  24.3 1.7 %collective-permute-done.14 = bf16[24,3200]{1,0:T(8,128)(2,1)S(1)} collective-permute-done((bf16[24,3200]{1,0:T(8,128)(2,1)S(1)}, bf16[24,3200]{1,0:T(8,128)(2,1)S(1)}, u32[]{:S(2)}, u32[]{:S(2)}) %collective-permute-start.14) | collective-permute-done | bytes 153632 | tf_op jit(solution)/shard_map/ppermute | solution.py:214
  26.1 1.2 %collective-permute-start.15 = (bf16[4,24,3200]{2,1,0:T(8,128)(2,1)S(1)}, bf16[4,24,3200]{2,1,0:T(8,128)(2,1)S(1)}, u32[]{:S(2)}, u32[]{:S(2)}) collective-permute-start(bf16[4,24,3200]{2,1,0:T(8,128)(2,1)S(1)} %pad_maximum_fusion.refs_7_), channel_id=1, source_target_pairs={{0,8},{8,16},{16,24},{24,0},{1,9},{9,17},{17,25},{25,1},{2,10},{10... | collective-permute-start | bytes 1843208 | tf_op jit(solution)/shard_map/ppermute | solution.py:214
  27.3 1.5 %collective-permute-start.16 = (bf16[4,24,3200]{2,1,0:T(8,128)(2,1)S(1)}, bf16[4,24,3200]{2,1,0:T(8,128)(2,1)S(1)}, u32[]{:S(2)}, u32[]{:S(2)}) collective-permute-start(bf16[4,24,3200]{2,1,0:T(8,128)(2,1)S(1)} %pad_maximum_fusion.refs_7_), channel_id=1, source_target_pairs={{0,24},{8,0},{16,8},{24,16},{1,25},{9,1},{17,9},{25,17},{2,26},{10... | collective-permute-start | bytes 1843208 | tf_op jit(solution)/shard_map/ppermute | solution.py:214
  28.9 1.4 %collective-permute-start.8 = (bf16[4,16,3200]{2,1,0:T(8,128)(2,1)S(1)}, bf16[4,16,3200]{2,1,0:T(8,128)(2,1)S(1)}, u32[]{:S(2)}, u32[]{:S(2)}) collective-permute-start(bf16[4,16,3200]{2,1,0:T(8,128)(2,1)S(1)} %pad_maximum_fusion.1.refs_6_), channel_id=1, source_target_pairs={{0,6},{2,0},{4,2},{6,4},{1,7},{3,1},{5,3},{7,5},{8,14},{10,8},{12,... | collective-permute-start | bytes 1228808 | tf_op jit(solution)/shard_map/ppermute | solution.py:214
  30.5 12.0 %collective-permute-done.15.refs_8_ = bf16[4,24,3200]{2,1,0:T(8,128)(2,1)S(1)} collective-permute-done((bf16[4,24,3200]{2,1,0:T(8,128)(2,1)S(1)}, bf16[4,24,3200]{2,1,0:T(8,128)(2,1)S(1)}, u32[]{:S(2)}, u32[]{:S(2)}) %collective-permute-start.15) | collective-permute-done | bytes 614432 | tf_op jit(solution)/shard_map/ppermute | solution.py:214
  42.7 2.7 %collective-permute-start.18 = (bf16[2,24,3200]{2,1,0:T(8,128)(2,1)S(1)}, bf16[2,24,3200]{2,1,0:T(8,128)(2,1)S(1)}, u32[]{:S(2)}, u32[]{:S(2)}) collective-permute-start(bf16[2,24,3200]{2,1,0:T(8,128)(2,1)S(1)} %slice.31), channel_id=1, source_target_pairs={{0,24},{8,0},{16,8},{24,16},{1,25},{9,1},{17,9},{25,17},{2,26},{10... | collective-permute-start | bytes 921608 | tf_op jit(solution)/shard_map/ppermute | solution.py:214
  45.3 0.7 collective-permute-start.10
  46.1 0.9 collective-permute-start.9
  47.0 3.0 %collective-permute-start = (s32[1,400]{1,0:T(1,128)S(1)}, s32[1,400]{1,0:T(1,128)S(1)}, u32[]{:S(2)}, u32[]{:S(2)}) collective-permute-start(s32[1,400]{1,0:T(1,128)S(1)} %copy-done.2), channel_id=1, source_target_pairs={{0,32},{32,0},{1,33},{33,1},{2,34},{34,2},{3,35},{35,3},{4,36},{36... | collective-permute-start | bytes 4808 | tf_op jit(solution)/shard_map/ppermute | solution.py:229
  50.0 0.8 collective-permute-done
  50.9 0.3 collective-permute-start.1
  51.1 4.2 %collective-permute-done.1.refs_1_ = s32[2,400]{1,0:T(2,128)S(1)} collective-permute-done((s32[2,400]{1,0:T(2,128)S(1)}, s32[2,400]{1,0:T(2,128)S(1)}, u32[]{:S(2)}, u32[]{:S(2)}) %collective-permute-start.1) | collective-permute-done | bytes 3232 | tf_op jit(solution)/shard_map/ppermute | solution.py:214
  55.4 3.4 %collective-permute-done.2.refs_2_ = s32[2,400]{1,0:T(2,128)S(1)} collective-permute-done((s32[2,400]{1,0:T(2,128)S(1)}, s32[2,400]{1,0:T(2,128)S(1)}, u32[]{:S(2)}, u32[]{:S(2)}) %collective-permute-start.2) | collective-permute-done | bytes 3232 | tf_op jit(solution)/shard_map/ppermute | solution.py:214
  58.8 2.4 %collective-permute-done.3.refs_3_ = s32[2,400]{1,0:T(2,128)S(1)} collective-permute-done((s32[2,400]{1,0:T(2,128)S(1)}, s32[2,400]{1,0:T(2,128)S(1)}, u32[]{:S(2)}, u32[]{:S(2)}) %collective-permute-start.3) | collective-permute-done | bytes 3232 | tf_op jit(solution)/shard_map/ppermute | solution.py:214
  61.2 7.7 %genes.1.refs_5_ = bf16[8,768,512]{2,1,0:T(8,128)(2,1)S(1)} custom-call(s32[2,400]{1,0:T(2,128)S(1)} %pad_add_fusion.refs_0_, s32[2,400]{1,0:T(2,128)S(1)} %collective-permute-done.1.refs_1_, s32[2,400]{1,0:T(2,128)S(1)} %collective-permute-done.2.refs_2_, s32[2,400]{1,0:T(2,128)S(1)} %collective-permute-done.3.refs_3_, bf16[750,3200]{1,0:T(8,128)(2,1)S(1)} %copy-done), custom_call_target="tpu_custom_call" | custom-call | tf_op jit(solution)/shard_map/genes/pallas_call | solution.py:98
  68.9 6.4 %shard_map.37.refs_6_ = f32[16,16,128]{2,1,0:T(8,128)S(1)} custom-call(s32[2,400]{1,0:T(2,128)S(1)} %pad_add_fusion.refs_0_, s32[2,400]{1,0:T(2,128)S(1)} %collective-permute-done.1.refs_1_, s32[2,400]{1,0:T(2,128)S(1)} %collective-permute-done.2.refs_2_, s32[2,400]{1,0:T(2,128)S(1)} %collective-permute-done.3.refs_3_, s32[1,750]{1,0:T(1,128)S(1)} %reshape.3.refs_4_, ...), custom_call_target="tpu_custom_call" | custom-call | tf_op jit(solution)/shard_map/pallas_call | solution.py:192
  75.3 8.5 %shard_map.38 = f32[16,40,128]{2,1,0:T(8,128)S(1)} custom-call(s32[2,400]{1,0:T(2,128)S(1)} %pad_add_fusion.refs_0_, s32[2,400]{1,0:T(2,128)S(1)} %collective-permute-done.1.refs_1_, s32[2,400]{1,0:T(2,128)S(1)} %collective-permute-done.2.refs_2_, s32[2,400]{1,0:T(2,128)S(1)} %collective-permute-done.3.refs_3_, s32[1,750]{1,0:T(1,128)S(1)} %reshape.3.refs_4_, ...), custom_call_target="tpu_custom_call" | custom-call | tf_op jit(solution)/shard_map/pallas_call | solution.py:192
  83.8 11.8 %all_to_all.5 = f32[16,40,128]{2,1,0:T(8,128)S(1)} all-to-all(f32[16,40,128]{2,1,0:T(8,128)S(1)} %shard_map.38), channel_id=1, replica_groups=mesh['z_lo'=4,'core'=2,'x'=4,'y'=4,'z_hi'=2] {'x','y'}, dimensions={0} | all-to-all | bytes 655360 | tf_op jit(solution)/shard_map/all_to_all | solution.py:242
  95.7 9.9 %collective-permute-start.19 = (f32[19,128]{1,0:T(8,128)S(1)}, f32[19,128]{1,0:T(8,128)S(1)}, u32[]{:S(2)}, u32[]{:S(2)}) collective-permute-start(f32[19,128]{1,0:T(8,128)S(1)} %get-tuple-element.12), channel_id=1, source_target_pairs={{0,0},{1,8},{2,16},{3,24},{4,32},{5,40},{6,48},{7,56},{8,64},{9,72... | collective-permute-start | bytes 29192 | tf_op jit(solution)/shard_map/ppermute | solution.py:251
  105.6 0.7 collective-permute-start.20
  106.4 8.7 %collective-permute-done.20 = f32[19,128]{1,0:T(8,128)S(1)} collective-permute-done((f32[19,128]{1,0:T(8,128)S(1)}, f32[19,128]{1,0:T(8,128)S(1)}, u32[]{:S(2)}, u32[]{:S(2)}) %collective-permute-start.20) | collective-permute-done | bytes 9760 | tf_op jit(solution)/shard_map/ppermute | solution.py:252
  115.1 0.6 add_log-plus-one_fusion
  (34 shorter events, 0.8 us)
Async XLA Ops:
  0.0 61.2 %copy-start = (bf16[750,3200]{1,0:T(8,128)(2,1)S(1)}, bf16[750,3200]{1,0:T(8,128)(2,1)}, u32[]{:S(2)}) copy-start(bf16[750,3200]{1,0:T(8,128)(2,1)} %refs_4_.1) | copy-start | bytes 14400004
  0.0 47.0 %copy-start.2 = (s32[1,400]{1,0:T(1,128)S(1)}, s32[1,400]{1,0:T(1,128)}, u32[]{:S(2)}) copy-start(s32[1,400]{1,0:T(1,128)} %param.4) | copy-start | bytes 4804
  0.0 58.8 %copy-start.1 = (s32[750]{0:T(1024)S(1)}, s32[750]{0:T(1024)}, u32[]{:S(2)}) copy-start(s32[750]{0:T(1024)} %param.5) | copy-start | bytes 9004
  1.7 13.8 %collective-permute-start.11 = (bf16[24,3200]{1,0:T(8,128)(2,1)S(1)}, bf16[24,3200]{1,0:T(8,128)(2,1)S(1)}, u32[]{:S(2)}, u32[]{:S(2)}) collective-permute-start(bf16[24,3200]{1,0:T(8,128)(2,1)S(1)} %get-tuple-element.10), channel_id=1, source_target_pairs={{0,193},{1,192},{64,129},{65,128},{128,65},{129,64},{192,1},{193,0... | collective-permute-start | bytes 460808 | tf_op jit(solution)/shard_map/ppermute | solution.py:231
  15.5 7.2 %collective-permute-start.12 = (bf16[24,3200]{1,0:T(8,128)(2,1)S(1)}, bf16[24,3200]{1,0:T(8,128)(2,1)S(1)}, u32[]{:S(2)}, u32[]{:S(2)}) collective-permute-start(bf16[24,3200]{1,0:T(8,128)(2,1)S(1)} %add.6), channel_id=1, source_target_pairs={{0,2},{2,4},{4,6},{6,0},{1,3},{3,5},{5,7},{7,1},{8,10},{10,12},{12... | collective-permute-start | bytes 460808 | tf_op jit(solution)/shard_map/ppermute | solution.py:214
  16.9 7.4 %collective-permute-start.13 = (bf16[24,3200]{1,0:T(8,128)(2,1)S(1)}, bf16[24,3200]{1,0:T(8,128)(2,1)S(1)}, u32[]{:S(2)}, u32[]{:S(2)}) collective-permute-start(bf16[24,3200]{1,0:T(8,128)(2,1)S(1)} %add.6), channel_id=1, source_target_pairs={{0,6},{2,0},{4,2},{6,4},{1,7},{3,1},{5,3},{7,5},{8,14},{10,8},{12,... | collective-permute-start | bytes 460808 | tf_op jit(solution)/shard_map/ppermute | solution.py:214
  18.5 7.5 %collective-permute-start.14 = (bf16[24,3200]{1,0:T(8,128)(2,1)S(1)}, bf16[24,3200]{1,0:T(8,128)(2,1)S(1)}, u32[]{:S(2)}, u32[]{:S(2)}) collective-permute-start(bf16[24,3200]{1,0:T(8,128)(2,1)S(1)} %add.6), channel_id=1, source_target_pairs={{0,4},{2,6},{4,0},{6,2},{1,5},{3,7},{5,1},{7,3},{8,12},{10,14},{12... | collective-permute-start | bytes 460808 | tf_op jit(solution)/shard_map/ppermute | solution.py:214
  20.0 8.8 %collective-permute-start.4 = (bf16[16,3200]{1,0:T(8,128)(2,1)S(1)}, bf16[16,3200]{1,0:T(8,128)(2,1)S(1)}, u32[]{:S(2)}, u32[]{:S(2)}) collective-permute-start(bf16[16,3200]{1,0:T(8,128)(2,1)S(1)} %get-tuple-element.8), channel_id=1, source_target_pairs={{0,8},{8,16},{16,24},{24,0},{1,9},{9,17},{17,25},{25,1},{2,10},{10... | collective-permute-start | bytes 307208 | tf_op jit(solution)/shard_map/ppermute | solution.py:214
  21.2 7.6 %collective-permute-start.5 = (bf16[16,3200]{1,0:T(8,128)(2,1)S(1)}, bf16[16,3200]{1,0:T(8,128)(2,1)S(1)}, u32[]{:S(2)}, u32[]{:S(2)}) collective-permute-start(bf16[16,3200]{1,0:T(8,128)(2,1)S(1)} %get-tuple-element.8), channel_id=1, source_target_pairs={{0,24},{8,0},{16,8},{24,16},{1,25},{9,1},{17,9},{25,17},{2,26},{10... | collective-permute-start | bytes 307208 | tf_op jit(solution)/shard_map/ppermute | solution.py:214
  22.7 6.2 %collective-permute-start.6 = (bf16[16,3200]{1,0:T(8,128)(2,1)S(1)}, bf16[16,3200]{1,0:T(8,128)(2,1)S(1)}, u32[]{:S(2)}, u32[]{:S(2)}) collective-permute-start(bf16[16,3200]{1,0:T(8,128)(2,1)S(1)} %get-tuple-element.8), channel_id=1, source_target_pairs={{0,16},{8,24},{16,0},{24,8},{1,17},{9,25},{17,1},{25,9},{2,18},{10... | collective-permute-start | bytes 307208 | tf_op jit(solution)/shard_map/ppermute | solution.py:214
  26.1 16.4 %collective-permute-start.15 = (bf16[4,24,3200]{2,1,0:T(8,128)(2,1)S(1)}, bf16[4,24,3200]{2,1,0:T(8,128)(2,1)S(1)}, u32[]{:S(2)}, u32[]{:S(2)}) collective-permute-start(bf16[4,24,3200]{2,1,0:T(8,128)(2,1)S(1)} %pad_maximum_fusion.refs_7_), channel_id=1, source_target_pairs={{0,8},{8,16},{16,24},{24,0},{1,9},{9,17},{17,25},{25,1},{2,10},{10... | collective-permute-start | bytes 1843208 | tf_op jit(solution)/shard_map/ppermute | solution.py:214
  27.3 15.3 %collective-permute-start.16 = (bf16[4,24,3200]{2,1,0:T(8,128)(2,1)S(1)}, bf16[4,24,3200]{2,1,0:T(8,128)(2,1)S(1)}, u32[]{:S(2)}, u32[]{:S(2)}) collective-permute-start(bf16[4,24,3200]{2,1,0:T(8,128)(2,1)S(1)} %pad_maximum_fusion.refs_7_), channel_id=1, source_target_pairs={{0,24},{8,0},{16,8},{24,16},{1,25},{9,1},{17,9},{25,17},{2,26},{10... | collective-permute-start | bytes 1843208 | tf_op jit(solution)/shard_map/ppermute | solution.py:214
  28.9 16.4 %collective-permute-start.8 = (bf16[4,16,3200]{2,1,0:T(8,128)(2,1)S(1)}, bf16[4,16,3200]{2,1,0:T(8,128)(2,1)S(1)}, u32[]{:S(2)}, u32[]{:S(2)}) collective-permute-start(bf16[4,16,3200]{2,1,0:T(8,128)(2,1)S(1)} %pad_maximum_fusion.1.refs_6_), channel_id=1, source_target_pairs={{0,6},{2,0},{4,2},{6,4},{1,7},{3,1},{5,3},{7,5},{8,14},{10,8},{12,... | collective-permute-start | bytes 1228808 | tf_op jit(solution)/shard_map/ppermute | solution.py:214
  30.4 15.7 %collective-permute-start.7 = (bf16[4,16,3200]{2,1,0:T(8,128)(2,1)S(1)}, bf16[4,16,3200]{2,1,0:T(8,128)(2,1)S(1)}, u32[]{:S(2)}, u32[]{:S(2)}) collective-permute-start(bf16[4,16,3200]{2,1,0:T(8,128)(2,1)S(1)} %pad_maximum_fusion.1.refs_6_), channel_id=1, source_target_pairs={{0,2},{2,4},{4,6},{6,0},{1,3},{3,5},{5,7},{7,1},{8,10},{10,12},{12... | collective-permute-start | bytes 1228808 | tf_op jit(solution)/shard_map/ppermute | solution.py:214
  42.5 32.8 %collective-permute-start.17 = (bf16[2,24,3200]{2,1,0:T(8,128)(2,1)S(1)}, bf16[2,24,3200]{2,1,0:T(8,128)(2,1)S(1)}, u32[]{:S(2)}, u32[]{:S(2)}) collective-permute-start(bf16[2,24,3200]{2,1,0:T(8,128)(2,1)S(1)} %slice.30), channel_id=1, source_target_pairs={{0,8},{8,16},{16,24},{24,0},{1,9},{9,17},{17,25},{25,1},{2,10},{10... | collective-permute-start | bytes 921608 | tf_op jit(solution)/shard_map/ppermute | solution.py:214
  42.7 32.7 %collective-permute-start.18 = (bf16[2,24,3200]{2,1,0:T(8,128)(2,1)S(1)}, bf16[2,24,3200]{2,1,0:T(8,128)(2,1)S(1)}, u32[]{:S(2)}, u32[]{:S(2)}) collective-permute-start(bf16[2,24,3200]{2,1,0:T(8,128)(2,1)S(1)} %slice.31), channel_id=1, source_target_pairs={{0,24},{8,0},{16,8},{24,16},{1,25},{9,1},{17,9},{25,17},{2,26},{10... | collective-permute-start | bytes 921608 | tf_op jit(solution)/shard_map/ppermute | solution.py:214
  45.3 23.6 %collective-permute-start.10 = (bf16[2,16,3200]{2,1,0:T(8,128)(2,1)S(1)}, bf16[2,16,3200]{2,1,0:T(8,128)(2,1)S(1)}, u32[]{:S(2)}, u32[]{:S(2)}) collective-permute-start(bf16[2,16,3200]{2,1,0:T(8,128)(2,1)S(1)} %slice.29), channel_id=1, source_target_pairs={{0,6},{2,0},{4,2},{6,4},{1,7},{3,1},{5,3},{7,5},{8,14},{10,8},{12,... | collective-permute-start | bytes 614408 | tf_op jit(solution)/shard_map/ppermute | solution.py:214
  46.1 22.8 %collective-permute-start.9 = (bf16[2,16,3200]{2,1,0:T(8,128)(2,1)S(1)}, bf16[2,16,3200]{2,1,0:T(8,128)(2,1)S(1)}, u32[]{:S(2)}, u32[]{:S(2)}) collective-permute-start(bf16[2,16,3200]{2,1,0:T(8,128)(2,1)S(1)} %slice.28), channel_id=1, source_target_pairs={{0,2},{2,4},{4,6},{6,0},{1,3},{3,5},{5,7},{7,1},{8,10},{10,12},{12... | collective-permute-start | bytes 614408 | tf_op jit(solution)/shard_map/ppermute | solution.py:214
  47.0 3.9 %collective-permute-start = (s32[1,400]{1,0:T(1,128)S(1)}, s32[1,400]{1,0:T(1,128)S(1)}, u32[]{:S(2)}, u32[]{:S(2)}) collective-permute-start(s32[1,400]{1,0:T(1,128)S(1)} %copy-done.2), channel_id=1, source_target_pairs={{0,32},{32,0},{1,33},{33,1},{2,34},{34,2},{3,35},{35,3},{4,36},{36... | collective-permute-start | bytes 4808 | tf_op jit(solution)/shard_map/ppermute | solution.py:229
  50.9 4.5 %collective-permute-start.1 = (s32[2,400]{1,0:T(2,128)S(1)}, s32[2,400]{1,0:T(2,128)S(1)}, u32[]{:S(2)}, u32[]{:S(2)}) collective-permute-start(s32[2,400]{1,0:T(2,128)S(1)} %pad_add_fusion.refs_0_), channel_id=1, source_target_pairs={{0,64},{64,128},{128,192},{192,0},{1,65},{65,129},{129,193},{193,1... | collective-permute-start | bytes 9608 | tf_op jit(solution)/shard_map/ppermute | solution.py:214
  55.4 3.4 %collective-permute-start.2 = (s32[2,400]{1,0:T(2,128)S(1)}, s32[2,400]{1,0:T(2,128)S(1)}, u32[]{:S(2)}, u32[]{:S(2)}) collective-permute-start(s32[2,400]{1,0:T(2,128)S(1)} %pad_add_fusion.refs_0_), channel_id=1, source_target_pairs={{0,128},{64,192},{128,0},{192,64},{1,129},{65,193},{129,1},{193,65... | collective-permute-start | bytes 9608 | tf_op jit(solution)/shard_map/ppermute | solution.py:214
  58.7 2.5 %collective-permute-start.3 = (s32[2,400]{1,0:T(2,128)S(1)}, s32[2,400]{1,0:T(2,128)S(1)}, u32[]{:S(2)}, u32[]{:S(2)}) collective-permute-start(s32[2,400]{1,0:T(2,128)S(1)} %pad_add_fusion.refs_0_), channel_id=1, source_target_pairs={{0,192},{64,0},{128,64},{192,128},{1,193},{65,1},{129,65},{193,129... | collective-permute-start | bytes 9608 | tf_op jit(solution)/shard_map/ppermute | solution.py:214
  95.7 10.7 %collective-permute-start.19 = (f32[19,128]{1,0:T(8,128)S(1)}, f32[19,128]{1,0:T(8,128)S(1)}, u32[]{:S(2)}, u32[]{:S(2)}) collective-permute-start(f32[19,128]{1,0:T(8,128)S(1)} %get-tuple-element.12), channel_id=1, source_target_pairs={{0,0},{1,8},{2,16},{3,24},{4,32},{5,40},{6,48},{7,56},{8,64},{9,72... | collective-permute-start | bytes 29192 | tf_op jit(solution)/shard_map/ppermute | solution.py:251
  105.6 9.5 %collective-permute-start.20 = (f32[19,128]{1,0:T(8,128)S(1)}, f32[19,128]{1,0:T(8,128)S(1)}, u32[]{:S(2)}, u32[]{:S(2)}) collective-permute-start(f32[19,128]{1,0:T(8,128)S(1)} %get-tuple-element.11), channel_id=1, source_target_pairs={{0,8},{1,0},{2,24},{3,16},{4,40},{5,32},{6,56},{7,48},{8,72},{9,64... | collective-permute-start | bytes 29192 | tf_op jit(solution)/shard_map/ppermute | solution.py:252
